TPU v7x, 256 devices: a whole 4x4x8 slice. The times are simulated.
256 devices in a mesh: row: 16 (over x, y), col: 16 (over z, core).
Axes of the slice: x: 4, y: 4, z: 8, core: 2. Of those that a mesh axis runs over, the one named last changes fastest.
Arguments:
- inputs: bfloat16 [2048, 16384], P('col', 'row'), may hold values from -6 to 6
- weight: bfloat16 [16384, 16384], P('row', 'col'), may hold values from -0.046875 to 0.046875
- cotangent: bfloat16 [2048, 16384], P('row', 'col'), may hold values from -0.75 to 0.75
- scale_in: float32 [8, 16384], P(None, 'row'), may hold values from -4 to 4
- scale_out: float32 [8, 16384], P(None, 'col'), may hold values from -4 to 4
- member: int32 [2048], replicated, may hold values from 0 to 7
Outputs:
- input_grad: bfloat16 [2048, 16384], P('col', 'row')
- weight_grad: float32 [16384, 16384], P('row', 'col')
- in_factor_grad: float32 [8, 16384], P(None, 'row')
- out_factor_grad: float32 [8, 16384], P(None, 'col')
All inputs are finite; a program needn't handle non-finite values.
Results may differ from a plain program's by a relative error of at most 0.0049.
Values may be sent and summed in bfloat16 or wider, within the bound.
No kernel may reach another device: no remote copies, remote signals or barrier semaphores. Data moves between devices by JAX's collectives and lax.ppermute only.
A program may use at most 128 MiB of HBM per device.

v0:
```python
import functools

import jax
import jax.numpy as jnp
from jax import lax
from jax.experimental import pallas as pl
from jax.experimental.pallas import tpu as pltpu
from jax.sharding import Mesh, PartitionSpec as P


NX, NY, NZ = 4, 4, 8
F32, BF16 = jnp.float32, jnp.bfloat16
PLANE = (0, -1, 1, 2)
LINE = (0, 1, 2, 6, 7, 3, 4, 5)
NEAR = 5


def ring(n, d):
    return [(i, (i + d) % n) for i in range(n)]


def shift(value, axis, n, d):
    return lax.ppermute(value, axis, ring(n, d))


def flip(value, axis, n, bit):
    return lax.ppermute(value, axis, [(i, i ^ bit) for i in range(n)])


def dot(a, b):
    return jnp.dot(a, b, preferred_element_type=F32)


def summed(hot_t, values):
    return dot(hot_t, values.astype(BF16))


def join_kernel(count, *refs):
    parts, outs = refs[:-count], refs[-count:]
    each = len(parts) // count
    for n, part in enumerate(parts):
        size = part.shape[0]
        outs[n // each][n % each * size : n % each * size + size, :] = part[...]


def stacks_kernel(*refs):
    for n in range(2):
        for m, part in enumerate(refs[4 * n : 4 * n + 4]):
            turned = (m + 2) % 4
            refs[8 + n][m * 64 : m * 64 + 64, :] = part[...]
            refs[10 + n][turned * 64 : turned * 64 + 64, :] = part[...]


def turn_kernel(weight, weight_t):
    for n in range(4):
        part = slice(n * 256, n * 256 + 256)
        weight_t[:, part] = weight[part, :].T


def back_kernel(fars, at, hot, factors, weight_t, *refs):
    stacks, (cot_all, scaled_all, own_other, pool) = refs[:-4], refs[-4:]
    x, y, z, c = at[0], at[1], at[2], at[3]
    row = 0
    for stack in stacks:
        if row < pool.shape[0]:
            pool[row : row + stack.shape[0], :] = stack[...]
            row += stack.shape[0]

    def stack_of(n, carry):
        turned = lax.rem(n, 2)
        far = fars[0]
        for m, other in enumerate(fars[1:]):
            far = jnp.where(n < 2 * m + 2, far, other)
        part = turned * 64
        starts, places = [], []
        for p, d in enumerate(PLANE):
            d = jnp.where(far == 1, PLANE[(p + 2) % 4], d)
            i = lax.rem(x + jnp.where(turned == 1, far, d) + 4, 4)
            j = lax.rem(y + jnp.where(turned == 1, d, far) + 4, 4)
            near = lax.rem(i * 2 + lax.div(j, 2) - z + 8, 8)
            spot = jnp.where(near < 3, near, jnp.where(near > 5, near - 3, near + 2))
            side = lax.rem(j + c, 2)
            starts.append(pl.multiple_of((spot * 2 + side) * 128 + part, 64))
            places.append(pl.multiple_of((side * 8 + spot) * 128 + part, 64))
        hots = jnp.concatenate([hot[pl.ds(s, 64), :] for s in starts], 0)
        values = pool[both(n), :]
        scaled = (values.astype(F32) * dot(hots, factors[...])).astype(BF16)
        back = dot(scaled, weight_t[...]).astype(BF16)
        for p in range(4):
            rows = slice(p * 64, p * 64 + 64)
            cot_all[pl.ds(starts[p], 64), :] = values[rows]
            scaled_all[pl.ds(starts[p], 64), :] = scaled[rows]
            own_other[pl.ds(places[p], 64), :] = back[rows]
        return carry

    lax.fori_loop(0, 2 * len(fars), stack_of, 0)


def block(n):
    return pl.ds(pl.multiple_of(n * 128, 128), 128)


def both(n):
    return pl.ds(pl.multiple_of(n * 256, 256), 256)


def in_kernel(hot_t, back, *refs):
    in_term = refs[-1]
    in_term[...] = jnp.zeros_like(in_term)
    for first, last, own, other in ((0, NEAR, *refs[:2]), (NEAR, NZ, *refs[2:4])):

        def chip(n, carry):
            values = jnp.concatenate([own[block(n - first), :], other[block(n - first), :]], 0)
            sums = jnp.concatenate([back[block(n), :], back[block(8 + n), :]], 0)
            in_term[...] += summed(hot_t[:, both(n)], values.astype(F32) * sums.astype(F32))
            return carry

        lax.fori_loop(first, last, chip, 0)


def front_kernel(first, hot, hot_t, factors, weight, cot_all, own, other, before, *outs):
    scaled_all, out_term = outs
    out_term[...] = before[...]

    def chip(n, carry):
        rows = both(first + n)
        values = jnp.concatenate([own[block(n), :], other[block(n), :]], 0).astype(F32)
        scaled = (values * dot(hot[rows, :], factors[...])).astype(BF16)
        scaled_all[both(n), :] = scaled
        product = cot_all[rows, :].astype(F32) * dot(scaled, weight[...])
        out_term[...] += summed(hot_t[:, rows], product)
        return carry

    lax.fori_loop(0, own.shape[0] // 128, chip, 0)


def grad_kernel(first, second, scaled_cot, *refs):
    split, grad = first.shape[0], refs[-1]
    grad[...] = sum(
        lax.dot_general(part[...], rows, (((0,), (0,)), ((), ())), preferred_element_type=F32)
        for part, rows in ((first, scaled_cot[:split, :]), (second, scaled_cot[split:, :]))
    )


def grad_part(first, second, scaled_cot, n, before=()):
    tiles = [pl.BlockSpec((p.shape[0], 256), lambda i: (0, i + 2 * n)) for p in (first, second)]
    return pl.pallas_call(
        grad_kernel,
        grid=(2,),
        out_shape=jax.ShapeDtypeStruct((1024, 1024), F32),
        in_specs=tiles
        + [pl.BlockSpec(memory_space=pltpu.VMEM)]
        + [pl.BlockSpec(memory_space=pl.ANY)] * len(before),
        out_specs=pl.BlockSpec((256, 1024), lambda i: (i + 2 * n, 0)),
        input_output_aliases={3: 0} if before else {},
        compiler_params=pltpu.CompilerParams(vmem_limit_bytes=16 * 2**20),
    )(first, second, scaled_cot, *before)


def call(kernel, outs, limit, *args, smem=0, aliases={}, scratch=()):
    vmem = pl.BlockSpec(memory_space=pltpu.VMEM)
    return pl.pallas_call(
        kernel,
        out_shape=[jax.ShapeDtypeStruct(*o) for o in outs],
        in_specs=[pl.BlockSpec(memory_space=pltpu.SMEM)] * smem + [vmem] * (len(args) - smem),
        out_specs=[vmem] * len(outs),
        input_output_aliases=aliases,
        scratch_shapes=scratch,
        compiler_params=pltpu.CompilerParams(vmem_limit_bytes=limit * 2**20),
    )(*args)


def thirds(factors):
    def cut(value):
        return lax.reduce_precision(value, 8, 7)

    high = cut(factors)
    middle = cut(factors - high)
    low = factors - high - middle
    parts = jnp.concatenate([high, middle, low], 0).astype(BF16)
    return jnp.pad(parts, ((0, 128 - parts.shape[0]), (0, 0)))


def step(inputs, weight, cotangent, scale_in, scale_out, member):
    a, b = cotangent[:64], cotangent[64:]
    a4 = [a] + [shift(a, "x", NX, -d) for d in PLANE[1:]]
    b4 = [b] + [shift(b, "y", NY, -d) for d in PLANE[1:]]
    stack = ((256, 1024), BF16)
    a4, b4, a4_back, b4_back = call(stacks_kernel, [stack] * 4, 8, *a4, *b4)
    (weight_t,) = call(turn_kernel, [((1024, 1024), BF16)], 8, weight)
    a4, b4, member, scale_in, scale_out = lax.optimization_barrier(
        (a4, b4, member, scale_in, scale_out)
    )

    def around(own, own_back, axis):
        before = shift(own, axis, 4, 1)
        after = shift(own_back, axis, 4, -1)
        far = (shift(before[:128], axis, 4, 1), shift(after[:128], axis, 4, -1))
        return before, after, far

    a_stacks, b_stacks = around(a4, a4_back, "y"), around(b4, b4_back, "x")

    at = jnp.stack([lax.axis_index(a) for a in ("x", "y", "z", "c")]).astype(jnp.int32)
    blocks = member.reshape(NZ, 2, 128)
    blocks = lax.dynamic_slice_in_dim(jnp.concatenate([blocks, blocks], 0), at[2], NZ, 0)
    blocks = jnp.where(at[3] == 0, blocks, blocks[:, ::-1])
    near = jnp.concatenate([blocks[:3], blocks[6:], blocks[3:6]], 0).reshape(-1)
    ids = jnp.arange(128, dtype=jnp.int32)
    hot = ((near[:, None] == (ids % 8)[None, :]) & (ids < 24)[None, :]).astype(BF16)
    hot_t = (near[None, :] == jnp.arange(16, dtype=jnp.int32)[:, None]).astype(BF16)
    s3, r3 = thirds(scale_out), thirds(scale_in)

    ups, downs = [inputs], [inputs]
    for _ in range(3):
        ups.append(shift(ups[-1], "z", NZ, 1))
        downs.append(shift(downs[-1], "z", NZ, -1))
    downs.append(shift(downs[-1], "z", NZ, -1))
    near_set = [inputs, downs[1], downs[2], ups[2], ups[1]]
    join = functools.partial(join_kernel, 1)
    (x_near,) = call(join, [((NEAR * 128, 1024), BF16)], 8, *near_set)
    (x_far,) = call(join, [((1024 - NEAR * 128, 1024), BF16)], 8, downs[3], downs[4], ups[3])
    held = [x_near, flip(x_near, "c", 2, 1), x_far, flip(x_far, "c", 2, 1)]

    whole, term = ((2048, 1024), BF16), ((16, 1024), F32)
    filled = ()
    for n, (fars, stacks) in enumerate((
        (PLANE[:1], (a4, b4)),
        (PLANE[1:3], (a_stacks[0], b_stacks[0], a_stacks[1], b_stacks[1])),
        (PLANE[3:], (*a_stacks[2], *b_stacks[2])),
    )):
        filled = call(
            functools.partial(back_kernel, fars), [whole, whole, whole], 12,
            at, hot, s3, weight_t, *stacks, *filled, smem=1,
            aliases={4 + len(stacks) + k: k for k in range(3)} if n else {},
            scratch=[pltpu.VMEM((len(fars) * 512, 1024), BF16)],
        )
    cot_all, scaled_cot, back = filled
    own = back[:1024]
    theirs = flip(back[1024:], "c", 2, 1)
    (in_term,) = call(in_kernel, [term], 8, hot_t, back, *held)

    def step_sum(n, arrived=None):
        first = LINE.index(n % 8) * 128
        part = slice(first, first + 128)
        if arrived is None:
            return (own[part].astype(F32) + theirs[part].astype(F32)).astype(BF16)
        arrived, ours, others = lax.optimization_barrier((arrived, own, theirs))
        total = ours[part].astype(F32) + others[part].astype(F32)
        return (total + arrived.astype(F32)).astype(BF16)

    right = shift(step_sum(4), "z", NZ, 1)
    left = shift(step_sum(-3), "z", NZ, -1)
    for n in (3, 2, 1):
        right = shift(step_sum(n, right), "z", NZ, 1)
        if n > 1:
            left = shift(step_sum(1 - n, left), "z", NZ, -1)
    back_block = own[:128].astype(F32) + theirs[:128].astype(F32)
    back_block = back_block + right.astype(F32) + left.astype(F32)
    input_grad = (back_block * dot(hot[:128], r3)).astype(BF16)

    out_term, scaled_in = jnp.zeros((16, 1024), F32), []
    for n, first in enumerate((0, NEAR)):
        parts = held[2 * n : 2 * n + 2]
        scaled, out_term = call(
            functools.partial(front_kernel, first),
            [((parts[0].shape[0] * 2, 1024), BF16), term], 10,
            hot, hot_t, r3, weight, cot_all, *parts, out_term,
        )
        scaled_in.append(scaled)
    weight_grad = grad_part(*scaled_in, scaled_cot, 0)
    weight_grad = grad_part(*scaled_in, scaled_cot, 1, (weight_grad,))
    in_term, out_term = in_term[:8], out_term[:8]
    in_term = in_term + flip(in_term, "c", 2, 1)
    for bit in (1, 2, 4):
        in_term = in_term + flip(in_term, "z", NZ, bit)
    for axis, bit in (("x", 1), ("y", 1), ("x", 2), ("y", 2)):
        out_term = out_term + flip(out_term, axis, 4, bit)
    return (input_grad, weight_grad, in_term, out_term)


def solution(mesh):
    fine = Mesh(mesh.devices.reshape(NX, NY, NZ, 2), ("x", "y", "z", "c"))
    row, col = ("x", "y"), ("z", "c")
    return jax.shard_map(
        step,
        mesh=fine,
        in_specs=(P(col, row), P(row, col), P(row, col), P(None, row), P(None, col), P()),
        out_specs=(P(col, row), P(row, col), P(None, row), P(None, col)),
        check_vma=False,
    )
```

profile of v0, /device:TPU:2, one launch (start us, length us, event | category | flops | bytes accessed | tf_op | source)
XLA Modules:
  0.0 139.2 jit_solution(1544465672152417673)
XLA Ops:
  0.6 1.0 fusion.19
  1.6 1.6 %collective-permute-start = (bf16[64,1024]{1,0:T(8,128)(2,1)S(1)}, bf16[64,1024]{1,0:T(8,128)(2,1)S(1)}, u32[]{:S(2)}, u32[]{:S(2)}) collective-permute-start(bf16[64,1024]{1,0:T(8,128)(2,1)S(1)} %get-tuple-element.83.refs_0_), channel_id=1, source_target_pairs={{0,64},{64,128},{128,192},{192,0},{1,65},{65,129},{129,193},{193,1... | collective-permute-start | bytes 393224 | tf_op jit(solution)/shard_map/ppermute | solution.py:23
  3.2 0.8 collective-permute-start.1
  4.0 2.0 %collective-permute-start.2 = (bf16[64,1024]{1,0:T(8,128)(2,1)S(1)}, bf16[64,1024]{1,0:T(8,128)(2,1)S(1)}, u32[]{:S(2)}, u32[]{:S(2)}) collective-permute-start(bf16[64,1024]{1,0:T(8,128)(2,1)S(1)} %get-tuple-element.83.refs_0_), channel_id=1, source_target_pairs={{0,128},{64,192},{128,0},{192,64},{1,129},{65,193},{129,1},{193,65... | collective-permute-start | bytes 393224 | tf_op jit(solution)/shard_map/ppermute | solution.py:23
  6.0 1.4 %collective-permute-start.3 = (bf16[64,1024]{1,0:T(8,128)(2,1)S(1)}, bf16[64,1024]{1,0:T(8,128)(2,1)S(1)}, u32[]{:S(2)}, u32[]{:S(2)}) collective-permute-start(bf16[64,1024]{1,0:T(8,128)(2,1)S(1)} %get-tuple-element.82.refs_4_), channel_id=1, source_target_pairs={{0,16},{16,32},{32,48},{48,0},{1,17},{17,33},{33,49},{49,1},{2,18}... | collective-permute-start | bytes 393224 | tf_op jit(solution)/shard_map/ppermute | solution.py:23
  7.4 1.8 %collective-permute-start.4 = (bf16[64,1024]{1,0:T(8,128)(2,1)S(1)}, bf16[64,1024]{1,0:T(8,128)(2,1)S(1)}, u32[]{:S(2)}, u32[]{:S(2)}) collective-permute-start(bf16[64,1024]{1,0:T(8,128)(2,1)S(1)} %get-tuple-element.82.refs_4_), channel_id=1, source_target_pairs={{0,48},{16,0},{32,16},{48,32},{1,49},{17,1},{33,17},{49,33},{2,50}... | collective-permute-start | bytes 393224 | tf_op jit(solution)/shard_map/ppermute | solution.py:23
  9.3 1.8 %collective-permute-start.5 = (bf16[64,1024]{1,0:T(8,128)(2,1)S(1)}, bf16[64,1024]{1,0:T(8,128)(2,1)S(1)}, u32[]{:S(2)}, u32[]{:S(2)}) collective-permute-start(bf16[64,1024]{1,0:T(8,128)(2,1)S(1)} %get-tuple-element.82.refs_4_), channel_id=1, source_target_pairs={{0,32},{16,48},{32,0},{48,16},{1,33},{17,49},{33,1},{49,17},{2,34}... | collective-permute-start | bytes 393224 | tf_op jit(solution)/shard_map/ppermute | solution.py:23
  11.1 0.5 iota_compare_fusion.2
  11.6 1.6 %copy-done = bf16[1024,1024]{1,0:T(8,128)(2,1)S(1)} copy-done((bf16[1024,1024]{1,0:T(8,128)(2,1)S(1)}, bf16[1024,1024]{1,0:T(8,128)(2,1)}, u32[]{:S(2)}) %copy-start) | copy-done | bytes 2097176
  13.2 0.6 shard_map.94.weight_t
  13.9 0.7 copy-done.3
  14.6 0.7 copy-done.5
  15.2 0.6 copy-done.7
  15.9 0.7 copy-done.9
  16.6 0.7 copy-done.11
  17.2 0.9 copy-done.4
  18.1 0.9 copy-done.6
  19.0 0.9 copy-done.8
  19.9 0.9 copy-done.10
  20.8 0.9 copy-done.12
  21.9 0.8 copy-done.13
  22.7 0.8 copy-done.14
  23.6 1.9 %collective-permute-start.10 = (bf16[256,1024]{1,0:T(8,128)(2,1)S(1)}, bf16[256,1024]{1,0:T(8,128)(2,1)S(1)}, u32[]{:S(2)}, u32[]{:S(2)}) collective-permute-start(bf16[256,1024]{1,0:T(8,128)(2,1)S(1)} %get-tuple-element.47.refs_1_), channel_id=1, source_target_pairs={{0,64},{64,128},{128,192},{192,0},{1,65},{65,129},{129,193},{193,1... | collective-permute-start | bytes 1572872 | tf_op jit(solution)/shard_map/ppermute | solution.py:23
  25.5 0.9 collective-permute-start.12
  26.4 2.6 %collective-permute-start.8 = (bf16[256,1024]{1,0:T(8,128)(2,1)}, bf16[256,1024]{1,0:T(8,128)(2,1)S(1)}, u32[]{:S(2)}, u32[]{:S(2)}) collective-permute-start(bf16[256,1024]{1,0:T(8,128)(2,1)} %copy-done.13), channel_id=1, source_target_pairs={{0,48},{16,0},{32,16},{48,32},{1,49},{17,1},{33,17},{49,33},{2,50}... | collective-permute-start | bytes 1572872 | tf_op jit(solution)/shard_map/ppermute | solution.py:23
  28.9 1.1 fusion.17
  30.0 5.6 %collective-permute-done.10.refs_1_ = bf16[256,1024]{1,0:T(8,128)(2,1)S(1)} collective-permute-done((bf16[256,1024]{1,0:T(8,128)(2,1)S(1)}, bf16[256,1024]{1,0:T(8,128)(2,1)S(1)}, u32[]{:S(2)}, u32[]{:S(2)}) %collective-permute-start.10) | collective-permute-done | bytes 524320 | tf_op jit(solution)/shard_map/ppermute | solution.py:23
  35.7 1.9 %collective-permute-start.11 = (bf16[128,1024]{1,0:T(8,128)(2,1)S(1)}, bf16[128,1024]{1,0:T(8,128)(2,1)S(1)}, u32[]{:S(2)}, u32[]{:S(2)}) collective-permute-start(bf16[128,1024]{1,0:T(8,128)(2,1)S(1)} %slice.128), channel_id=1, source_target_pairs={{0,64},{64,128},{128,192},{192,0},{1,65},{65,129},{129,193},{193,1... | collective-permute-start | bytes 786440 | tf_op jit(solution)/shard_map/ppermute | solution.py:23
  37.8 1.5 %collective-permute-start.13 = (bf16[128,1024]{1,0:T(8,128)(2,1)S(1)}, bf16[128,1024]{1,0:T(8,128)(2,1)S(1)}, u32[]{:S(2)}, u32[]{:S(2)}) collective-permute-start(bf16[128,1024]{1,0:T(8,128)(2,1)S(1)} %slice.129), channel_id=1, source_target_pairs={{0,192},{64,0},{128,64},{192,128},{1,193},{65,1},{129,65},{193,129... | collective-permute-start | bytes 786440 | tf_op jit(solution)/shard_map/ppermute | solution.py:23
  39.3 3.0 %collective-permute-start.9 = (bf16[128,1024]{1,0:T(8,128)(2,1)S(1)}, bf16[128,1024]{1,0:T(8,128)(2,1)S(1)}, u32[]{:S(2)}, u32[]{:S(2)}) collective-permute-start(bf16[128,1024]{1,0:T(8,128)(2,1)S(1)} %slice.127), channel_id=1, source_target_pairs={{0,48},{16,0},{32,16},{48,32},{1,49},{17,1},{33,17},{49,33},{2,50}... | collective-permute-start | bytes 786440 | tf_op jit(solution)/shard_map/ppermute | solution.py:23
  42.3 0.8 reduce-precision_convert_fusion.1
  43.2 2.3 %shard_map.95 = (bf16[2048,1024]{1,0:T(8,128)(2,1)S(1)}, bf16[2048,1024]{1,0:T(8,128)(2,1)S(1)}, bf16[2048,1024]{1,0:T(8,128)(2,1)S(1)}) custom-call(s32[4]{0:T(128)S(1)} %pad_add_fusion.1.at, bf16[2048,128]{1,0:T(8,128)(2,1)S(1)} %get-tuple-element.90.hot, bf16[128,1024]{1,0:T(8,128)(2,1)S(1)} %fusion.7.factors, bf16[1024,1024]{1,0:T(8,128)(2,1)S(1)} %shard_map.94.weight_t, ...), custom_call_target="tpu_custom_call" | custom-call | tf_op jit(solution)/shard_map/pallas_call | solution.py:162
  45.5 4.1 %shard_map.96 = (bf16[2048,1024]{1,0:T(8,128)(2,1)S(1)}, bf16[2048,1024]{1,0:T(8,128)(2,1)S(1)}, bf16[2048,1024]{1,0:T(8,128)(2,1)S(1)}) custom-call(s32[4]{0:T(128)S(1)} %pad_add_fusion.1.at, bf16[2048,128]{1,0:T(8,128)(2,1)S(1)} %get-tuple-element.90.hot, ...), custom_call_target="tpu_custom_call", output_to_operand_aliasing={{0}: (8, {}), {1}: (9, {}), {2}: (10, {})} | custom-call | tf_op jit(solution)/shard_map/pallas_call | solution.py:162
  49.7 2.3 %shard_map.97 = (bf16[2048,1024]{1,0:T(8,128)(2,1)S(1)}, bf16[2048,1024]{1,0:T(8,128)(2,1)S(1)}, bf16[2048,1024]{1,0:T(8,128)(2,1)S(1)}) custom-call(s32[4]{0:T(128)S(1)} %pad_add_fusion.1.at, bf16[2048,128]{1,0:T(8,128)(2,1)S(1)} %get-tuple-element.90.hot, ...), custom_call_target="tpu_custom_call", output_to_operand_aliasing={{0}: (8, {}), {1}: (9, {}), {2}: (10, {})} | custom-call | tf_op jit(solution)/shard_map/pallas_call | solution.py:162
  52.0 0.4 fusion.18
  52.6 0.4 copy-done.2
  53.0 5.9 %collective-permute-start.22 = (bf16[128,1024]{1,0:T(8,128)(2,1)S(1)}, bf16[128,1024]{1,0:T(8,128)(2,1)S(1)}, u32[]{:S(2)}, u32[]{:S(2)}) collective-permute-start(bf16[128,1024]{1,0:T(8,128)(2,1)S(1)} %copy-done.2), channel_id=1, source_target_pairs={{0,14},{2,0},{4,2},{6,4},{8,6},{10,8},{12,10},{14,12},{1,15},{3,1}... | collective-permute-start | bytes 786440 | tf_op jit(solution)/shard_map/ppermute | solution.py:23
  58.8 5.8 %collective-permute-done.22.refs_1_ = bf16[128,1024]{1,0:T(8,128)(2,1)S(1)} collective-permute-done((bf16[128,1024]{1,0:T(8,128)(2,1)S(1)}, bf16[128,1024]{1,0:T(8,128)(2,1)S(1)}, u32[]{:S(2)}, u32[]{:S(2)}) %collective-permute-start.22) | collective-permute-done | bytes 262176 | tf_op jit(solution)/shard_map/ppermute | solution.py:23
  64.7 3.7 %collective-permute-start.23 = (bf16[128,1024]{1,0:T(8,128)(2,1)S(1)}, bf16[128,1024]{1,0:T(8,128)(2,1)S(1)}, u32[]{:S(2)}, u32[]{:S(2)}) collective-permute-start(bf16[128,1024]{1,0:T(8,128)(2,1)S(1)} %collective-permute-done.22.refs_1_), channel_id=1, source_target_pairs={{0,14},{2,0},{4,2},{6,4},{8,6},{10,8},{12,10},{14,12},{1,15},{3,1}... | collective-permute-start | bytes 786440 | tf_op jit(solution)/shard_map/ppermute | solution.py:23
  68.4 5.0 %collective-permute-done.23.refs_2_ = bf16[128,1024]{1,0:T(8,128)(2,1)S(1)} collective-permute-done((bf16[128,1024]{1,0:T(8,128)(2,1)S(1)}, bf16[128,1024]{1,0:T(8,128)(2,1)S(1)}, u32[]{:S(2)}, u32[]{:S(2)}) %collective-permute-start.23) | collective-permute-done | bytes 262176 | tf_op jit(solution)/shard_map/ppermute | solution.py:23
  73.3 3.7 %collective-permute-start.27 = (bf16[128,1024]{1,0:T(8,128)(2,1)S(1)}, bf16[128,1024]{1,0:T(8,128)(2,1)S(1)}, u32[]{:S(2)}, u32[]{:S(2)}) collective-permute-start(bf16[128,1024]{1,0:T(8,128)(2,1)S(1)} %collective-permute-done.23.refs_2_), channel_id=1, source_target_pairs={{0,14},{2,0},{4,2},{6,4},{8,6},{10,8},{12,10},{14,12},{1,15},{3,1}... | collective-permute-start | bytes 786440 | tf_op jit(solution)/shard_map/ppermute | solution.py:23
  77.3 3.8 %collective-permute-done.27.refs_0_ = bf16[128,1024]{1,0:T(8,128)(2,1)S(1)} collective-permute-done((bf16[128,1024]{1,0:T(8,128)(2,1)S(1)}, bf16[128,1024]{1,0:T(8,128)(2,1)S(1)}, u32[]{:S(2)}, u32[]{:S(2)}) %collective-permute-start.27) | collective-permute-done | bytes 262176 | tf_op jit(solution)/shard_map/ppermute | solution.py:23
  81.2 3.7 %collective-permute-start.28 = (bf16[128,1024]{1,0:T(8,128)(2,1)S(1)}, bf16[128,1024]{1,0:T(8,128)(2,1)S(1)}, u32[]{:S(2)}, u32[]{:S(2)}) collective-permute-start(bf16[128,1024]{1,0:T(8,128)(2,1)S(1)} %collective-permute-done.27.refs_0_), channel_id=1, source_target_pairs={{0,14},{2,0},{4,2},{6,4},{8,6},{10,8},{12,10},{14,12},{1,15},{3,1}... | collective-permute-start | bytes 786440 | tf_op jit(solution)/shard_map/ppermute | solution.py:23
  84.9 2.3 %collective-permute-done.29.refs_2_ = bf16[128,1024]{1,0:T(8,128)(2,1)S(1)} collective-permute-done((bf16[128,1024]{1,0:T(8,128)(2,1)S(1)}, bf16[128,1024]{1,0:T(8,128)(2,1)S(1)}, u32[]{:S(2)}, u32[]{:S(2)}) %collective-permute-start.29) | collective-permute-done | bytes 262176 | tf_op jit(solution)/shard_map/ppermute | solution.py:23
  87.2 1.6 %collective-permute-done.28.refs_1_ = bf16[128,1024]{1,0:T(8,128)(2,1)S(1)} collective-permute-done((bf16[128,1024]{1,0:T(8,128)(2,1)S(1)}, bf16[128,1024]{1,0:T(8,128)(2,1)S(1)}, u32[]{:S(2)}, u32[]{:S(2)}) %collective-permute-start.28) | collective-permute-done | bytes 262176 | tf_op jit(solution)/shard_map/ppermute | solution.py:23
  89.3 4.8 %shard_map.99 = (bf16[1280,1024]{1,0:T(8,128)(2,1)S(1)}, f32[16,1024]{1,0:T(8,128)S(1)}) custom-call(bf16[2048,128]{1,0:T(8,128)(2,1)S(1)} %get-tuple-element.90.hot, bf16[16,2048]{1,0:T(8,128)(2,1)S(1)} %fusion.10.hot_t, bf16[128,1024]{1,0:T(8,128)(2,1)S(1)} %fusion.9.factors, bf16[1024,1024]{1,0:T(8,128)(2,1)S(1)} %copy-done.1, ...), custom_call_target="tpu_custom_call" | custom-call | tf_op jit(solution)/shard_map/pallas_call | solution.py:162
  94.1 2.9 %shard_map.101 = (bf16[768,1024]{1,0:T(8,128)(2,1)S(1)}, f32[16,1024]{1,0:T(8,128)S(1)}) custom-call(bf16[2048,128]{1,0:T(8,128)(2,1)S(1)} %get-tuple-element.90.hot, bf16[16,2048]{1,0:T(8,128)(2,1)S(1)} %fusion.10.hot_t, bf16[128,1024]{1,0:T(8,128)(2,1)S(1)} %fusion.9.factors, bf16[1024,1024]{1,0:T(8,128)(2,1)S(1)} %copy-done.1, ...), custom_call_target="tpu_custom_call" | custom-call | tf_op jit(solution)/shard_map/pallas_call | solution.py:162
  97.0 3.3 %collective-permute-start.35 = (f32[8,1024]{1,0:T(8,128)S(1)}, f32[8,1024]{1,0:T(8,128)S(1)}, u32[]{:S(2)}, u32[]{:S(2)}) collective-permute-start(f32[8,1024]{1,0:T(8,128)S(1)} %slice.122), channel_id=1, source_target_pairs={{0,64},{64,0},{128,192},{192,128},{1,65},{65,1},{129,193},{193,129... | collective-permute-start | bytes 98312 | tf_op jit(solution)/shard_map/ppermute | solution.py:27
  100.3 2.2 %shard_map.104 = f32[16,1024]{1,0:T(8,128)S(1)} custom-call(bf16[16,2048]{1,0:T(8,128)(2,1)S(1)} %fusion.10.hot_t, bf16[2048,1024]{1,0:T(8,128)(2,1)S(1)} %get-tuple-element.55.back, bf16[640,1024]{1,0:T(8,128)(2,1)S(1)} %shard_map.98.own.refs_0_, bf16[640,1024]{1,0:T(8,128)(2,1)S(1)} %collective-permute-done.26.other.refs_1_, ...), custom_call_target="tpu_custom_call" | custom-call | tf_op jit(solution)/shard_map/pallas_call | solution.py:162
  102.5 0.3 collective-permute-start.31
  102.9 3.8 %collective-permute-start.19 = (bf16[128,1024]{1,0:T(8,128)(2,1)S(1)}, bf16[128,1024]{1,0:T(8,128)(2,1)S(1)}, u32[]{:S(2)}, u32[]{:S(2)}) collective-permute-start(bf16[128,1024]{1,0:T(8,128)(2,1)S(1)} %get-tuple-element.79), channel_id=1, source_target_pairs={{0,14},{2,0},{4,2},{6,4},{8,6},{10,8},{12,10},{14,12},{1,15},{3,1}... | collective-permute-start | bytes 786440 | tf_op jit(solution)/shard_map/ppermute | solution.py:23
  106.9 0.3 collective-permute-start.32
  107.2 5.4 %collective-permute-done.19 = bf16[128,1024]{1,0:T(8,128)(2,1)S(1)} collective-permute-done((bf16[128,1024]{1,0:T(8,128)(2,1)S(1)}, bf16[128,1024]{1,0:T(8,128)(2,1)S(1)}, u32[]{:S(2)}, u32[]{:S(2)}) %collective-permute-start.19) | collective-permute-done | bytes 262176 | tf_op jit(solution)/shard_map/ppermute | solution.py:23
  112.8 3.8 %collective-permute-start.20 = (bf16[128,1024]{1,0:T(8,128)(2,1)S(1)}, bf16[128,1024]{1,0:T(8,128)(2,1)S(1)}, u32[]{:S(2)}, u32[]{:S(2)}) collective-permute-start(bf16[128,1024]{1,0:T(8,128)(2,1)S(1)} %add_convert_fusion.1), channel_id=1, source_target_pairs={{0,14},{2,0},{4,2},{6,4},{8,6},{10,8},{12,10},{14,12},{1,15},{3,1}... | collective-permute-start | bytes 786440 | tf_op jit(solution)/shard_map/ppermute | solution.py:23
  116.9 1.1 collective-permute-start.33
  118.0 3.7 %collective-permute-done.20 = bf16[128,1024]{1,0:T(8,128)(2,1)S(1)} collective-permute-done((bf16[128,1024]{1,0:T(8,128)(2,1)S(1)}, bf16[128,1024]{1,0:T(8,128)(2,1)S(1)}, u32[]{:S(2)}, u32[]{:S(2)}) %collective-permute-start.20) | collective-permute-done | bytes 262176 | tf_op jit(solution)/shard_map/ppermute | solution.py:23
  121.9 3.8 %collective-permute-start.21 = (bf16[128,1024]{1,0:T(8,128)(2,1)S(1)}, bf16[128,1024]{1,0:T(8,128)(2,1)S(1)}, u32[]{:S(2)}, u32[]{:S(2)}) collective-permute-start(bf16[128,1024]{1,0:T(8,128)(2,1)S(1)} %add_convert_fusion), channel_id=1, source_target_pairs={{0,14},{2,0},{4,2},{6,4},{8,6},{10,8},{12,10},{14,12},{1,15},{3,1}... | collective-permute-start | bytes 786440 | tf_op jit(solution)/shard_map/ppermute | solution.py:23
  125.9 1.1 collective-permute-start.38
  127.0 2.1 %collective-permute-start.34 = (f32[8,1024]{1,0:T(8,128)S(1)}, f32[8,1024]{1,0:T(8,128)S(1)}, u32[]{:S(2)}, u32[]{:S(2)}) collective-permute-start(f32[8,1024]{1,0:T(8,128)S(1)} %add.105), channel_id=1, source_target_pairs={{0,8},{2,10},{4,12},{6,14},{8,0},{10,2},{12,4},{14,6},{1,9},{3,11}... | collective-permute-start | bytes 98312 | tf_op jit(solution)/shard_map/ppermute | solution.py:27
  129.3 3.9 %shard_map.102.refs_0_ = f32[1024,1024]{1,0:T(8,128)} custom-call(bf16[1280,1024]{1,0:T(8,128)(2,1)S(1)} %get-tuple-element.73.first, bf16[768,1024]{1,0:T(8,128)(2,1)S(1)} %get-tuple-element.75.second, bf16[2048,1024]{1,0:T(8,128)(2,1)S(1)} %get-tuple-element.76.scaled_cot), custom_call_target="tpu_custom_call" | custom-call | tf_op jit(solution)/shard_map/pallas_call | solution.py:147
  133.2 3.9 %shard_map.103 = f32[1024,1024]{1,0:T(8,128)} custom-call(bf16[1280,1024]{1,0:T(8,128)(2,1)S(1)} %get-tuple-element.73.first, bf16[768,1024]{1,0:T(8,128)(2,1)S(1)} %get-tuple-element.75.second, bf16[2048,1024]{1,0:T(8,128)(2,1)S(1)} %get-tuple-element.76.scaled_cot, f32[1024,1024]{1,0:T(8,128)} %shard_map.102.refs_0_), custom_call_target="tpu_custom_call", output_to_operand_aliasing={{}: (3, {})} | custom-call | tf_op jit(solution)/shard_map/pallas_call | solution.py:147
  137.1 0.6 add.110
  137.7 0.6 add.106
  138.3 0.9 multiply_convert_fusion
  (97 shorter events, 2.8 us)
Async XLA Ops:
  1.6 7.6 %collective-permute-start = (bf16[64,1024]{1,0:T(8,128)(2,1)S(1)}, bf16[64,1024]{1,0:T(8,128)(2,1)S(1)}, u32[]{:S(2)}, u32[]{:S(2)}) collective-permute-start(bf16[64,1024]{1,0:T(8,128)(2,1)S(1)} %get-tuple-element.83.refs_0_), channel_id=1, source_target_pairs={{0,64},{64,128},{128,192},{192,0},{1,65},{65,129},{129,193},{193,1... | collective-permute-start | bytes 393224 | tf_op jit(solution)/shard_map/ppermute | solution.py:23
  3.2 10.7 %collective-permute-start.1 = (bf16[64,1024]{1,0:T(8,128)(2,1)S(1)}, bf16[64,1024]{1,0:T(8,128)(2,1)S(1)}, u32[]{:S(2)}, u32[]{:S(2)}) collective-permute-start(bf16[64,1024]{1,0:T(8,128)(2,1)S(1)} %get-tuple-element.83.refs_0_), channel_id=1, source_target_pairs={{0,192},{64,0},{128,64},{192,128},{1,193},{65,1},{129,65},{193,129... | collective-permute-start | bytes 393224 | tf_op jit(solution)/shard_map/ppermute | solution.py:23
  4.0 10.5 %collective-permute-start.2 = (bf16[64,1024]{1,0:T(8,128)(2,1)S(1)}, bf16[64,1024]{1,0:T(8,128)(2,1)S(1)}, u32[]{:S(2)}, u32[]{:S(2)}) collective-permute-start(bf16[64,1024]{1,0:T(8,128)(2,1)S(1)} %get-tuple-element.83.refs_0_), channel_id=1, source_target_pairs={{0,128},{64,192},{128,0},{192,64},{1,129},{65,193},{129,1},{193,65... | collective-permute-start | bytes 393224 | tf_op jit(solution)/shard_map/ppermute | solution.py:23
  6.0 9.2 %collective-permute-start.3 = (bf16[64,1024]{1,0:T(8,128)(2,1)S(1)}, bf16[64,1024]{1,0:T(8,128)(2,1)S(1)}, u32[]{:S(2)}, u32[]{:S(2)}) collective-permute-start(bf16[64,1024]{1,0:T(8,128)(2,1)S(1)} %get-tuple-element.82.refs_4_), channel_id=1, source_target_pairs={{0,16},{16,32},{32,48},{48,0},{1,17},{17,33},{33,49},{49,1},{2,18}... | collective-permute-start | bytes 393224 | tf_op jit(solution)/shard_map/ppermute | solution.py:23
  7.4 8.5 %collective-permute-start.4 = (bf16[64,1024]{1,0:T(8,128)(2,1)S(1)}, bf16[64,1024]{1,0:T(8,128)(2,1)S(1)}, u32[]{:S(2)}, u32[]{:S(2)}) collective-permute-start(bf16[64,1024]{1,0:T(8,128)(2,1)S(1)} %get-tuple-element.82.refs_4_), channel_id=1, source_target_pairs={{0,48},{16,0},{32,16},{48,32},{1,49},{17,1},{33,17},{49,33},{2,50}... | collective-permute-start | bytes 393224 | tf_op jit(solution)/shard_map/ppermute | solution.py:23
  9.3 7.3 %collective-permute-start.5 = (bf16[64,1024]{1,0:T(8,128)(2,1)S(1)}, bf16[64,1024]{1,0:T(8,128)(2,1)S(1)}, u32[]{:S(2)}, u32[]{:S(2)}) collective-permute-start(bf16[64,1024]{1,0:T(8,128)(2,1)S(1)} %get-tuple-element.82.refs_4_), channel_id=1, source_target_pairs={{0,32},{16,48},{32,0},{48,16},{1,33},{17,49},{33,1},{49,17},{2,34}... | collective-permute-start | bytes 393224 | tf_op jit(solution)/shard_map/ppermute | solution.py:23
  11.6 1.6 %copy-start = (bf16[1024,1024]{1,0:T(8,128)(2,1)S(1)}, bf16[1024,1024]{1,0:T(8,128)(2,1)}, u32[]{:S(2)}) copy-start(bf16[1024,1024]{1,0:T(8,128)(2,1)} %weight.5) | copy-start | bytes 6291460
  13.2 10.3 %copy-start.15 = (s32[2048]{0:T(1024)S(1)}, s32[2048]{0:T(1024)}, u32[]{:S(2)}) copy-start(s32[2048]{0:T(1024)} %param.11) | copy-start | bytes 24580
  13.9 0.7 copy-start.3
  14.6 0.7 copy-start.5
  15.2 0.7 copy-start.7
  15.9 0.7 copy-start.9
  16.5 0.7 copy-start.11
  17.2 0.9 copy-start.4
  18.1 0.9 copy-start.6
  19.0 0.9 copy-start.8
  19.9 0.9 copy-start.10
  20.8 0.9 copy-start.12
  21.9 0.8 copy-start.13
  22.7 0.8 copy-start.14
  23.6 12.1 %collective-permute-start.10 = (bf16[256,1024]{1,0:T(8,128)(2,1)S(1)}, bf16[256,1024]{1,0:T(8,128)(2,1)S(1)}, u32[]{:S(2)}, u32[]{:S(2)}) collective-permute-start(bf16[256,1024]{1,0:T(8,128)(2,1)S(1)} %get-tuple-element.47.refs_1_), channel_id=1, source_target_pairs={{0,64},{64,128},{128,192},{192,0},{1,65},{65,129},{129,193},{193,1... | collective-permute-start | bytes 1572872 | tf_op jit(solution)/shard_map/ppermute | solution.py:23
  25.5 12.2 %collective-permute-start.6 = (bf16[256,1024]{1,0:T(8,128)(2,1)S(1)}, bf16[256,1024]{1,0:T(8,128)(2,1)S(1)}, u32[]{:S(2)}, u32[]{:S(2)}) collective-permute-start(bf16[256,1024]{1,0:T(8,128)(2,1)S(1)} %get-tuple-element.45.refs_0_), channel_id=1, source_target_pairs={{0,16},{16,32},{32,48},{48,0},{1,17},{17,33},{33,49},{49,1},{2,18}... | collective-permute-start | bytes 1572872 | tf_op jit(solution)/shard_map/ppermute | solution.py:23
  25.5 12.3 %collective-permute-start.12 = (bf16[256,1024]{1,0:T(8,128)(2,1)}, bf16[256,1024]{1,0:T(8,128)(2,1)S(1)}, u32[]{:S(2)}, u32[]{:S(2)}) collective-permute-start(bf16[256,1024]{1,0:T(8,128)(2,1)} %copy-done.14), channel_id=1, source_target_pairs={{0,192},{64,0},{128,64},{192,128},{1,193},{65,1},{129,65},{193,129... | collective-permute-start | bytes 1572872 | tf_op jit(solution)/shard_map/ppermute | solution.py:23
  26.4 12.9 %collective-permute-start.8 = (bf16[256,1024]{1,0:T(8,128)(2,1)}, bf16[256,1024]{1,0:T(8,128)(2,1)S(1)}, u32[]{:S(2)}, u32[]{:S(2)}) collective-permute-start(bf16[256,1024]{1,0:T(8,128)(2,1)} %copy-done.13), channel_id=1, source_target_pairs={{0,48},{16,0},{32,16},{48,32},{1,49},{17,1},{33,17},{49,33},{2,50}... | collective-permute-start | bytes 1572872 | tf_op jit(solution)/shard_map/ppermute | solution.py:23
  35.7 14.0 %collective-permute-start.11 = (bf16[128,1024]{1,0:T(8,128)(2,1)S(1)}, bf16[128,1024]{1,0:T(8,128)(2,1)S(1)}, u32[]{:S(2)}, u32[]{:S(2)}) collective-permute-start(bf16[128,1024]{1,0:T(8,128)(2,1)S(1)} %slice.128), channel_id=1, source_target_pairs={{0,64},{64,128},{128,192},{192,0},{1,65},{65,129},{129,193},{193,1... | collective-permute-start | bytes 786440 | tf_op jit(solution)/shard_map/ppermute | solution.py:23
  37.7 12.0 %collective-permute-start.7 = (bf16[128,1024]{1,0:T(8,128)(2,1)S(1)}, bf16[128,1024]{1,0:T(8,128)(2,1)S(1)}, u32[]{:S(2)}, u32[]{:S(2)}) collective-permute-start(bf16[128,1024]{1,0:T(8,128)(2,1)S(1)} %slice.126), channel_id=1, source_target_pairs={{0,16},{16,32},{32,48},{48,0},{1,17},{17,33},{33,49},{49,1},{2,18}... | collective-permute-start | bytes 786440 | tf_op jit(solution)/shard_map/ppermute | solution.py:23
  37.8 11.8 %collective-permute-start.13 = (bf16[128,1024]{1,0:T(8,128)(2,1)S(1)}, bf16[128,1024]{1,0:T(8,128)(2,1)S(1)}, u32[]{:S(2)}, u32[]{:S(2)}) collective-permute-start(bf16[128,1024]{1,0:T(8,128)(2,1)S(1)} %slice.129), channel_id=1, source_target_pairs={{0,192},{64,0},{128,64},{192,128},{1,193},{65,1},{129,65},{193,129... | collective-permute-start | bytes 786440 | tf_op jit(solution)/shard_map/ppermute | solution.py:23
  39.3 10.3 %collective-permute-start.9 = (bf16[128,1024]{1,0:T(8,128)(2,1)S(1)}, bf16[128,1024]{1,0:T(8,128)(2,1)S(1)}, u32[]{:S(2)}, u32[]{:S(2)}) collective-permute-start(bf16[128,1024]{1,0:T(8,128)(2,1)S(1)} %slice.127), channel_id=1, source_target_pairs={{0,48},{16,0},{32,16},{48,32},{1,49},{17,1},{33,17},{49,33},{2,50}... | collective-permute-start | bytes 786440 | tf_op jit(solution)/shard_map/ppermute | solution.py:23
  52.0 1.0 copy-start.2
  52.5 36.4 %collective-permute-start.14 = (bf16[1024,1024]{1,0:T(8,128)(2,1)S(1)}, bf16[1024,1024]{1,0:T(8,128)(2,1)S(1)}, u32[]{:S(2)}, u32[]{:S(2)}) collective-permute-start(bf16[1024,1024]{1,0:T(8,128)(2,1)S(1)} %get-tuple-element.81), channel_id=1, source_target_pairs={{0,1},{1,0},{2,3},{3,2},{4,5},{5,4},{6,7},{7,6},{8,9},{9,8},{10,11... | collective-permute-start | bytes 6291464 | tf_op jit(solution)/shard_map/ppermute | solution.py:27
  53.0 11.7 %collective-permute-start.22 = (bf16[128,1024]{1,0:T(8,128)(2,1)S(1)}, bf16[128,1024]{1,0:T(8,128)(2,1)S(1)}, u32[]{:S(2)}, u32[]{:S(2)}) collective-permute-start(bf16[128,1024]{1,0:T(8,128)(2,1)S(1)} %copy-done.2), channel_id=1, source_target_pairs={{0,14},{2,0},{4,2},{6,4},{8,6},{10,8},{12,10},{14,12},{1,15},{3,1}... | collective-permute-start | bytes 786440 | tf_op jit(solution)/shard_map/ppermute | solution.py:23
  58.8 9.5 %collective-permute-start.24 = (bf16[128,1024]{1,0:T(8,128)(2,1)S(1)}, bf16[128,1024]{1,0:T(8,128)(2,1)S(1)}, u32[]{:S(2)}, u32[]{:S(2)}) collective-permute-start(bf16[128,1024]{1,0:T(8,128)(2,1)S(1)} %copy-done.2), channel_id=1, source_target_pairs={{0,2},{2,4},{4,6},{6,8},{8,10},{10,12},{12,14},{14,0},{1,3},{3,5},... | collective-permute-start | bytes 786440 | tf_op jit(solution)/shard_map/ppermute | solution.py:23
  64.7 8.7 %collective-permute-start.23 = (bf16[128,1024]{1,0:T(8,128)(2,1)S(1)}, bf16[128,1024]{1,0:T(8,128)(2,1)S(1)}, u32[]{:S(2)}, u32[]{:S(2)}) collective-permute-start(bf16[128,1024]{1,0:T(8,128)(2,1)S(1)} %collective-permute-done.22.refs_1_), channel_id=1, source_target_pairs={{0,14},{2,0},{4,2},{6,4},{8,6},{10,8},{12,10},{14,12},{1,15},{3,1}... | collective-permute-start | bytes 786440 | tf_op jit(solution)/shard_map/ppermute | solution.py:23
  68.4 8.7 %collective-permute-start.25 = (bf16[128,1024]{1,0:T(8,128)(2,1)S(1)}, bf16[128,1024]{1,0:T(8,128)(2,1)S(1)}, u32[]{:S(2)}, u32[]{:S(2)}) collective-permute-start(bf16[128,1024]{1,0:T(8,128)(2,1)S(1)} %collective-permute-done.24.refs_4_), channel_id=1, source_target_pairs={{0,2},{2,4},{4,6},{6,8},{8,10},{10,12},{12,14},{14,0},{1,3},{3,5},... | collective-permute-start | bytes 786440 | tf_op jit(solution)/shard_map/ppermute | solution.py:23
  73.3 7.8 %collective-permute-start.27 = (bf16[128,1024]{1,0:T(8,128)(2,1)S(1)}, bf16[128,1024]{1,0:T(8,128)(2,1)S(1)}, u32[]{:S(2)}, u32[]{:S(2)}) collective-permute-start(bf16[128,1024]{1,0:T(8,128)(2,1)S(1)} %collective-permute-done.23.refs_2_), channel_id=1, source_target_pairs={{0,14},{2,0},{4,2},{6,4},{8,6},{10,8},{12,10},{14,12},{1,15},{3,1}... | collective-permute-start | bytes 786440 | tf_op jit(solution)/shard_map/ppermute | solution.py:23
  77.1 12.1 %copy-start.1 = (bf16[1024,1024]{1,0:T(8,128)(2,1)S(1)}, bf16[1024,1024]{1,0:T(8,128)(2,1)}, u32[]{:S(2)}) copy-start(bf16[1024,1024]{1,0:T(8,128)(2,1)} %weight.5) | copy-start | bytes 6291460
  77.1 12.1 %collective-permute-start.26 = (bf16[640,1024]{1,0:T(8,128)(2,1)S(1)}, bf16[640,1024]{1,0:T(8,128)(2,1)S(1)}, u32[]{:S(2)}, u32[]{:S(2)}) collective-permute-start(bf16[640,1024]{1,0:T(8,128)(2,1)S(1)} %shard_map.98.own.refs_0_), channel_id=1, source_target_pairs={{0,1},{1,0},{2,3},{3,2},{4,5},{5,4},{6,7},{7,6},{8,9},{9,8},{10,11... | collective-permute-start | bytes 3932168 | tf_op jit(solution)/shard_map/ppermute | solution.py:27
  77.2 9.9 %collective-permute-start.29 = (bf16[128,1024]{1,0:T(8,128)(2,1)S(1)}, bf16[128,1024]{1,0:T(8,128)(2,1)S(1)}, u32[]{:S(2)}, u32[]{:S(2)}) collective-permute-start(bf16[128,1024]{1,0:T(8,128)(2,1)S(1)} %collective-permute-done.25.refs_3_), channel_id=1, source_target_pairs={{0,2},{2,4},{4,6},{6,8},{8,10},{10,12},{12,14},{14,0},{1,3},{3,5},... | collective-permute-start | bytes 786440 | tf_op jit(solution)/shard_map/ppermute | solution.py:23
  81.2 7.6 %collective-permute-start.28 = (bf16[128,1024]{1,0:T(8,128)(2,1)S(1)}, bf16[128,1024]{1,0:T(8,128)(2,1)S(1)}, u32[]{:S(2)}, u32[]{:S(2)}) collective-permute-start(bf16[128,1024]{1,0:T(8,128)(2,1)S(1)} %collective-permute-done.27.refs_0_), channel_id=1, source_target_pairs={{0,14},{2,0},{4,2},{6,4},{8,6},{10,8},{12,10},{14,12},{1,15},{3,1}... | collective-permute-start | bytes 786440 | tf_op jit(solution)/shard_map/ppermute | solution.py:23
  88.8 5.3 %collective-permute-start.30 = (bf16[384,1024]{1,0:T(8,128)(2,1)S(1)}, bf16[384,1024]{1,0:T(8,128)(2,1)S(1)}, u32[]{:S(2)}, u32[]{:S(2)}) collective-permute-start(bf16[384,1024]{1,0:T(8,128)(2,1)S(1)} %shard_map.100.own.refs_2_), channel_id=1, source_target_pairs={{0,1},{1,0},{2,3},{3,2},{4,5},{5,4},{6,7},{7,6},{8,9},{9,8},{10,11... | collective-permute-start | bytes 2359304 | tf_op jit(solution)/shard_map/ppermute | solution.py:27
  89.1 17.5 %collective-permute-start.15 = (bf16[128,1024]{1,0:T(8,128)(2,1)S(1)}, bf16[128,1024]{1,0:T(8,128)(2,1)S(1)}, u32[]{:S(2)}, u32[]{:S(2)}) collective-permute-start(bf16[128,1024]{1,0:T(8,128)(2,1)S(1)} %get-tuple-element.78), channel_id=1, source_target_pairs={{0,2},{2,4},{4,6},{6,8},{8,10},{10,12},{12,14},{14,0},{1,3},{3,5},... | collective-permute-start | bytes 786440 | tf_op jit(solution)/shard_map/ppermute | solution.py:23
  97.0 5.7 %collective-permute-start.35 = (f32[8,1024]{1,0:T(8,128)S(1)}, f32[8,1024]{1,0:T(8,128)S(1)}, u32[]{:S(2)}, u32[]{:S(2)}) collective-permute-start(f32[8,1024]{1,0:T(8,128)S(1)} %slice.122), channel_id=1, source_target_pairs={{0,64},{64,0},{128,192},{192,128},{1,65},{65,1},{129,193},{193,129... | collective-permute-start | bytes 98312 | tf_op jit(solution)/shard_map/ppermute | solution.py:27
  102.5 4.4 %collective-permute-start.31 = (f32[8,1024]{1,0:T(8,128)S(1)}, f32[8,1024]{1,0:T(8,128)S(1)}, u32[]{:S(2)}, u32[]{:S(2)}) collective-permute-start(f32[8,1024]{1,0:T(8,128)S(1)} %slice.134), channel_id=1, source_target_pairs={{0,1},{1,0},{2,3},{3,2},{4,5},{5,4},{6,7},{7,6},{8,9},{9,8},{10,11... | collective-permute-start | bytes 98312 | tf_op jit(solution)/shard_map/ppermute | solution.py:27
  102.8 14.0 %collective-permute-start.36 = (f32[8,1024]{1,0:T(8,128)S(1)}, f32[8,1024]{1,0:T(8,128)S(1)}, u32[]{:S(2)}, u32[]{:S(2)}) collective-permute-start(f32[8,1024]{1,0:T(8,128)S(1)} %slice_add_fusion.1), channel_id=1, source_target_pairs={{0,16},{16,0},{32,48},{48,32},{1,17},{17,1},{33,49},{49,33},{2,18}... | collective-permute-start | bytes 98312 | tf_op jit(solution)/shard_map/ppermute | solution.py:27
  102.9 9.8 %collective-permute-start.19 = (bf16[128,1024]{1,0:T(8,128)(2,1)S(1)}, bf16[128,1024]{1,0:T(8,128)(2,1)S(1)}, u32[]{:S(2)}, u32[]{:S(2)}) collective-permute-start(bf16[128,1024]{1,0:T(8,128)(2,1)S(1)} %get-tuple-element.79), channel_id=1, source_target_pairs={{0,14},{2,0},{4,2},{6,4},{8,6},{10,8},{12,10},{14,12},{1,15},{3,1}... | collective-permute-start | bytes 786440 | tf_op jit(solution)/shard_map/ppermute | solution.py:23
  106.8 9.8 %collective-permute-start.16 = (bf16[128,1024]{1,0:T(8,128)(2,1)S(1)}, bf16[128,1024]{1,0:T(8,128)(2,1)S(1)}, u32[]{:S(2)}, u32[]{:S(2)}) collective-permute-start(bf16[128,1024]{1,0:T(8,128)(2,1)S(1)} %add_convert_fusion.5), channel_id=1, source_target_pairs={{0,2},{2,4},{4,6},{6,8},{8,10},{10,12},{12,14},{14,0},{1,3},{3,5},... | collective-permute-start | bytes 786440 | tf_op jit(solution)/shard_map/ppermute | solution.py:23
  106.9 10.0 %collective-permute-start.32 = (f32[8,1024]{1,0:T(8,128)S(1)}, f32[8,1024]{1,0:T(8,128)S(1)}, u32[]{:S(2)}, u32[]{:S(2)}) collective-permute-start(f32[8,1024]{1,0:T(8,128)S(1)} %slice_add_fusion), channel_id=1, source_target_pairs={{0,2},{2,0},{4,6},{6,4},{8,10},{10,8},{12,14},{14,12},{1,3},{3,1},... | collective-permute-start | bytes 98312 | tf_op jit(solution)/shard_map/ppermute | solution.py:27
  112.8 8.9 %collective-permute-start.20 = (bf16[128,1024]{1,0:T(8,128)(2,1)S(1)}, bf16[128,1024]{1,0:T(8,128)(2,1)S(1)}, u32[]{:S(2)}, u32[]{:S(2)}) collective-permute-start(bf16[128,1024]{1,0:T(8,128)(2,1)S(1)} %add_convert_fusion.1), channel_id=1, source_target_pairs={{0,14},{2,0},{4,2},{6,4},{8,6},{10,8},{12,10},{14,12},{1,15},{3,1}... | collective-permute-start | bytes 786440 | tf_op jit(solution)/shard_map/ppermute | solution.py:23
  116.7 8.9 %collective-permute-start.17 = (bf16[128,1024]{1,0:T(8,128)(2,1)S(1)}, bf16[128,1024]{1,0:T(8,128)(2,1)S(1)}, u32[]{:S(2)}, u32[]{:S(2)}) collective-permute-start(bf16[128,1024]{1,0:T(8,128)(2,1)S(1)} %add_convert_fusion.4), channel_id=1, source_target_pairs={{0,2},{2,4},{4,6},{6,8},{8,10},{10,12},{12,14},{14,0},{1,3},{3,5},... | collective-permute-start | bytes 786440 | tf_op jit(solution)/shard_map/ppermute | solution.py:23
  116.8 9.1 %collective-permute-start.37 = (f32[8,1024]{1,0:T(8,128)S(1)}, f32[8,1024]{1,0:T(8,128)S(1)}, u32[]{:S(2)}, u32[]{:S(2)}) collective-permute-start(f32[8,1024]{1,0:T(8,128)S(1)} %add.108), channel_id=1, source_target_pairs={{0,128},{64,192},{128,0},{192,64},{1,129},{65,193},{129,1},{193,65... | collective-permute-start | bytes 98312 | tf_op jit(solution)/shard_map/ppermute | solution.py:27
  116.9 10.1 %collective-permute-start.33 = (f32[8,1024]{1,0:T(8,128)S(1)}, f32[8,1024]{1,0:T(8,128)S(1)}, u32[]{:S(2)}, u32[]{:S(2)}) collective-permute-start(f32[8,1024]{1,0:T(8,128)S(1)} %add.104), channel_id=1, source_target_pairs={{0,4},{2,6},{4,0},{6,2},{8,12},{10,14},{12,8},{14,10},{1,5},{3,7},... | collective-permute-start | bytes 98312 | tf_op jit(solution)/shard_map/ppermute | solution.py:27
  121.9 16.4 %collective-permute-start.21 = (bf16[128,1024]{1,0:T(8,128)(2,1)S(1)}, bf16[128,1024]{1,0:T(8,128)(2,1)S(1)}, u32[]{:S(2)}, u32[]{:S(2)}) collective-permute-start(bf16[128,1024]{1,0:T(8,128)(2,1)S(1)} %add_convert_fusion), channel_id=1, source_target_pairs={{0,14},{2,0},{4,2},{6,4},{8,6},{10,8},{12,10},{14,12},{1,15},{3,1}... | collective-permute-start | bytes 786440 | tf_op jit(solution)/shard_map/ppermute | solution.py:23
  125.8 12.5 %collective-permute-start.18 = (bf16[128,1024]{1,0:T(8,128)(2,1)S(1)}, bf16[128,1024]{1,0:T(8,128)(2,1)S(1)}, u32[]{:S(2)}, u32[]{:S(2)}) collective-permute-start(bf16[128,1024]{1,0:T(8,128)(2,1)S(1)} %add_convert_fusion.3), channel_id=1, source_target_pairs={{0,2},{2,4},{4,6},{6,8},{8,10},{10,12},{12,14},{14,0},{1,3},{3,5},... | collective-permute-start | bytes 786440 | tf_op jit(solution)/shard_map/ppermute | solution.py:23
  125.9 11.2 %collective-permute-start.38 = (f32[8,1024]{1,0:T(8,128)S(1)}, f32[8,1024]{1,0:T(8,128)S(1)}, u32[]{:S(2)}, u32[]{:S(2)}) collective-permute-start(f32[8,1024]{1,0:T(8,128)S(1)} %add.109), channel_id=1, source_target_pairs={{0,32},{16,48},{32,0},{48,16},{1,33},{17,49},{33,1},{49,17},{2,34}... | collective-permute-start | bytes 98312 | tf_op jit(solution)/shard_map/ppermute | solution.py:27
  127.0 10.7 %collective-permute-start.34 = (f32[8,1024]{1,0:T(8,128)S(1)}, f32[8,1024]{1,0:T(8,128)S(1)}, u32[]{:S(2)}, u32[]{:S(2)}) collective-permute-start(f32[8,1024]{1,0:T(8,128)S(1)} %add.105), channel_id=1, source_target_pairs={{0,8},{2,10},{4,12},{6,14},{8,0},{10,2},{12,4},{14,6},{1,9},{3,11}... | collective-permute-start | bytes 98312 | tf_op jit(solution)/shard_map/ppermute | solution.py:27
where the time goes:
time: 140 us; the launch traced here: 139 us
  starting transfers between devices  58.5 us (42%)
  waiting for transfers between devices  33.5 us (24%)
  Pallas kernels  27.4 us (20%)
  local copies, waits for them, and re-layouts  12.9 us (9%)
  other arithmetic  5.57 us (4%)
    ppermute x28, starting transfers between devices, shift(): return lax.ppermute(value, axis, ring(n, d))  49.9 us
    ppermute x28, waiting for transfers between devices, shift(): return lax.ppermute(value, axis, ring(n, d))  33.4 us
    pallas_call x10, Pallas kernels, call(): pl.pallas_call(kernel, out_shape=[jax.ShapeDtypeStruct(*o) for o in outs]...  19.6 us
    unnamed x32, local copies, waits for them, and re-layouts  11.4 us
    ppermute x11, starting transfers between devices, flip(): return lax.ppermute(value, axis, [(i, i ^ bit) for i in range(n)])  8.64 us
    pallas_call x2, Pallas kernels, grad_part(): pl.pallas_call(grad_kernel, grid=(2,), out_shape=jax.ShapeDtypeStruct((10...  7.74 us
  transfers between devices with their start and end apart: 39, of which 9 were waited for; matrix products, arithmetic and copies ran while one was open for 4% of the time, Pallas kernels for 18%

commit v1 on v0

--- a/solution.py
+++ b/solution.py
@@ -51,10 +51,26 @@
             refs[10 + n][turned * 64 : turned * 64 + 64, :] = part[...]
 
 
-def turn_kernel(weight, weight_t):
+def turn_kernel(at, member, scale_in, scale_out, weight, weight_t, hot, hot_t, r3, s3):
     for n in range(4):
         part = slice(n * 256, n * 256 + 256)
         weight_t[:, part] = weight[part, :].T
+    z, c = at[2], at[3]
+    ids = lax.broadcasted_iota(jnp.int32, (128, 128), 0)
+    for n, near in enumerate(LINE):
+        for side in range(2):
+            k = lax.rem(z + near, 8) * 2 + lax.rem(side + c, 2)
+            here = jnp.broadcast_to(member[pl.ds(k, 1), :], (128, 128))
+            part = slice((2 * n + side) * 128, (2 * n + side) * 128 + 128)
+            match = jnp.where((here == lax.rem(ids, 8)) & (ids < 24), 1.0, 0.0)
+            hot[part, :] = match.T.astype(BF16)
+            hot_t[:, part] = jnp.where(here[:16] == ids[:16], 1.0, 0.0).astype(BF16)
+    for factors, out in ((scale_in, r3), (scale_out, s3)):
+        value = factors[...]
+        high = value.astype(BF16).astype(F32)
+        middle = (value - high).astype(BF16).astype(F32)
+        parts = [high, middle, value - high - middle, jnp.zeros((104, 1024), F32)]
+        out[...] = jnp.concatenate(parts, 0).astype(BF16)
 
 
 def back_kernel(fars, at, hot, factors, weight_t, *refs):
@@ -157,28 +173,19 @@
     )(first, second, scaled_cot, *before)
 
 
-def call(kernel, outs, limit, *args, smem=0, aliases={}, scratch=()):
+def call(kernel, outs, limit, *args, smem=0, aliases={}, scratch=(), fetch=False):
     vmem = pl.BlockSpec(memory_space=pltpu.VMEM)
+    ins = [pl.BlockSpec(a.shape, lambda i: (0, 0)) if fetch else vmem for a in args[smem:]]
     return pl.pallas_call(
         kernel,
+        grid=(1,) if fetch else (),
         out_shape=[jax.ShapeDtypeStruct(*o) for o in outs],
-        in_specs=[pl.BlockSpec(memory_space=pltpu.SMEM)] * smem + [vmem] * (len(args) - smem),
+        in_specs=[pl.BlockSpec(memory_space=pltpu.SMEM)] * smem + ins,
         out_specs=[vmem] * len(outs),
         input_output_aliases=aliases,
         scratch_shapes=scratch,
         compiler_params=pltpu.CompilerParams(vmem_limit_bytes=limit * 2**20),
     )(*args)
-
-
-def thirds(factors):
-    def cut(value):
-        return lax.reduce_precision(value, 8, 7)
-
-    high = cut(factors)
-    middle = cut(factors - high)
-    low = factors - high - middle
-    parts = jnp.concatenate([high, middle, low], 0).astype(BF16)
-    return jnp.pad(parts, ((0, 128 - parts.shape[0]), (0, 0)))
 
 
 def step(inputs, weight, cotangent, scale_in, scale_out, member):
@@ -187,9 +194,12 @@
     b4 = [b] + [shift(b, "y", NY, -d) for d in PLANE[1:]]
     stack = ((256, 1024), BF16)
     a4, b4, a4_back, b4_back = call(stacks_kernel, [stack] * 4, 8, *a4, *b4)
-    (weight_t,) = call(turn_kernel, [((1024, 1024), BF16)], 8, weight)
-    a4, b4, member, scale_in, scale_out = lax.optimization_barrier(
-        (a4, b4, member, scale_in, scale_out)
+    at = jnp.stack([lax.axis_index(a) for a in ("x", "y", "z", "c")]).astype(jnp.int32)
+    weight_t, hot, hot_t, r3, s3 = call(
+        turn_kernel,
+        [((1024, 1024), BF16), ((2048, 128), BF16), ((16, 2048), BF16)] + [((128, 1024), BF16)] * 2,
+        12, at, member.reshape(16, 128), scale_in, scale_out, weight, smem=1,
+        fetch=True,
     )
 
     def around(own, own_back, axis):
@@ -199,16 +209,6 @@
         return before, after, far
 
     a_stacks, b_stacks = around(a4, a4_back, "y"), around(b4, b4_back, "x")
-
-    at = jnp.stack([lax.axis_index(a) for a in ("x", "y", "z", "c")]).astype(jnp.int32)
-    blocks = member.reshape(NZ, 2, 128)
-    blocks = lax.dynamic_slice_in_dim(jnp.concatenate([blocks, blocks], 0), at[2], NZ, 0)
-    blocks = jnp.where(at[3] == 0, blocks, blocks[:, ::-1])
-    near = jnp.concatenate([blocks[:3], blocks[6:], blocks[3:6]], 0).reshape(-1)
-    ids = jnp.arange(128, dtype=jnp.int32)
-    hot = ((near[:, None] == (ids % 8)[None, :]) & (ids < 24)[None, :]).astype(BF16)
-    hot_t = (near[None, :] == jnp.arange(16, dtype=jnp.int32)[:, None]).astype(BF16)
-    s3, r3 = thirds(scale_out), thirds(scale_in)
 
     ups, downs = [inputs], [inputs]
     for _ in range(3):

time: 140 us -> 142 us (1.014)
  waiting for transfers between devices: 33.5 us -> 49 us
  starting transfers between devices: 58.5 us -> 52.2 us
  local copies, waits for them, and re-layouts: 12.9 us -> 7.32 us
  other arithmetic: 5.57 us -> 3.05 us
    ppermute x28, waiting for transfers between devices: 33.4 us -> 49 us  [shift(): return lax.ppermute(value, axis, ring(n, d))]
    unnamed x32 -> x26, local copies, waits for them, and re-layouts: 11.4 us -> 2.83 us
    ppermute x28, starting transfers between devices: 49.9 us -> 44.8 us  [shift(): return lax.ppermute(value, axis, ring(n, d))]
    slice x4, local copies, waits for them, and re-layouts: 0.07 us -> 2.91 us  [around(): far = (shift(before[:128], axis, 4, 1), shift(after[:128], axis, 4, -1))]
  transfers between devices with their start and end apart: 39 -> 39, of which waited for: 9 -> 13; matrix products, arithmetic and copies ran while one was open for 4% -> 4% of each run, Pallas kernels for 18% -> 18%
where the time goes in v1:
time: 142 us
  starting transfers between devices  52.2 us (37%)
  waiting for transfers between devices  49 us (35%)
  Pallas kernels  28.8 us (20%)
  local copies, waits for them, and re-layouts  7.32 us (5%)
  other arithmetic  3.05 us (2%)
    ppermute x28, waiting for transfers between devices, shift(): return lax.ppermute(value, axis, ring(n, d))  49 us
    ppermute x28, starting transfers between devices, shift(): return lax.ppermute(value, axis, ring(n, d))  44.8 us
    pallas_call x10, Pallas kernels, call(): pl.pallas_call(kernel, grid=(1,) if fetch else (), out_shape=[jax.ShapeDt...  21 us
    pallas_call x2, Pallas kernels, grad_part(): pl.pallas_call(grad_kernel, grid=(2,), out_shape=jax.ShapeDtypeStruct((10...  7.75 us
    ppermute x11, starting transfers between devices, flip(): return lax.ppermute(value, axis, [(i, i ^ bit) for i in range(n)])  7.37 us
    slice x4, local copies, waits for them, and re-layouts, around(): far = (shift(before[:128], axis, 4, 1), shift(after[:128], axis, 4, -1))  2.91 us
  transfers between devices with their start and end apart: 39, of which 13 were waited for; matrix products, arithmetic and copies ran while one was open for 4% of the time, Pallas kernels for 18%

profile of v1, /device:TPU:2, one launch (start us, length us, event | category | flops | bytes accessed | tf_op | source)
XLA Modules:
  0.0 141.7 jit_solution(15275658910493039388)
XLA Ops:
  0.7 1.1 fusion.3
  1.8 1.6 %collective-permute-start = (bf16[64,1024]{1,0:T(8,128)(2,1)S(1)}, bf16[64,1024]{1,0:T(8,128)(2,1)S(1)}, u32[]{:S(2)}, u32[]{:S(2)}) collective-permute-start(bf16[64,1024]{1,0:T(8,128)(2,1)S(1)} %get-tuple-element.83.refs_0_), channel_id=1, source_target_pairs={{0,64},{64,128},{128,192},{192,0},{1,65},{65,129},{129,193},{193,1... | collective-permute-start | bytes 393224 | tf_op jit(solution)/shard_map/ppermute | solution.py:23
  3.4 0.8 collective-permute-start.1
  4.2 2.0 %collective-permute-start.2 = (bf16[64,1024]{1,0:T(8,128)(2,1)S(1)}, bf16[64,1024]{1,0:T(8,128)(2,1)S(1)}, u32[]{:S(2)}, u32[]{:S(2)}) collective-permute-start(bf16[64,1024]{1,0:T(8,128)(2,1)S(1)} %get-tuple-element.83.refs_0_), channel_id=1, source_target_pairs={{0,128},{64,192},{128,0},{192,64},{1,129},{65,193},{129,1},{193,65... | collective-permute-start | bytes 393224 | tf_op jit(solution)/shard_map/ppermute | solution.py:23
  6.2 1.4 collective-permute-start.3
  7.6 1.8 %collective-permute-start.4 = (bf16[64,1024]{1,0:T(8,128)(2,1)S(1)}, bf16[64,1024]{1,0:T(8,128)(2,1)S(1)}, u32[]{:S(2)}, u32[]{:S(2)}) collective-permute-start(bf16[64,1024]{1,0:T(8,128)(2,1)S(1)} %get-tuple-element.82.refs_4_), channel_id=1, source_target_pairs={{0,48},{16,0},{32,16},{48,32},{1,49},{17,1},{33,17},{49,33},{2,50}... | collective-permute-start | bytes 393224 | tf_op jit(solution)/shard_map/ppermute | solution.py:23
  9.4 1.8 %collective-permute-start.5 = (bf16[64,1024]{1,0:T(8,128)(2,1)S(1)}, bf16[64,1024]{1,0:T(8,128)(2,1)S(1)}, u32[]{:S(2)}, u32[]{:S(2)}) collective-permute-start(bf16[64,1024]{1,0:T(8,128)(2,1)S(1)} %get-tuple-element.82.refs_4_), channel_id=1, source_target_pairs={{0,32},{16,48},{32,0},{48,16},{1,33},{17,49},{33,1},{49,17},{2,34}... | collective-permute-start | bytes 393224 | tf_op jit(solution)/shard_map/ppermute | solution.py:23
  11.3 0.5 collective-permute-done.2.refs_3_
  11.8 1.3 collective-permute-done.3.refs_5_
  13.1 0.7 collective-permute-done.4.refs_6_
  13.8 2.3 %collective-permute-done.5.refs_7_ = bf16[64,1024]{1,0:T(8,128)(2,1)S(1)} collective-permute-done((bf16[64,1024]{1,0:T(8,128)(2,1)S(1)}, bf16[64,1024]{1,0:T(8,128)(2,1)S(1)}, u32[]{:S(2)}, u32[]{:S(2)}) %collective-permute-start.5) | collective-permute-done | bytes 131104 | tf_op jit(solution)/shard_map/ppermute | solution.py:23
  16.1 0.1 shard_map.94
  16.2 2.5 %collective-permute-start.10 = (bf16[256,1024]{1,0:T(8,128)(2,1)S(1)}, bf16[256,1024]{1,0:T(8,128)(2,1)S(1)}, u32[]{:S(2)}, u32[]{:S(2)}) collective-permute-start(bf16[256,1024]{1,0:T(8,128)(2,1)S(1)} %get-tuple-element.46.refs_1_), channel_id=1, source_target_pairs={{0,64},{64,128},{128,192},{192,0},{1,65},{65,129},{129,193},{193,1... | collective-permute-start | bytes 1572872 | tf_op jit(solution)/shard_map/ppermute | solution.py:23
  18.8 0.8 copy-done.7
  19.6 0.3 collective-permute-start.12
  19.9 2.9 %collective-permute-start.8 = (bf16[256,1024]{1,0:T(8,128)(2,1)S(1)}, bf16[256,1024]{1,0:T(8,128)(2,1)S(1)}, u32[]{:S(2)}, u32[]{:S(2)}) collective-permute-start(bf16[256,1024]{1,0:T(8,128)(2,1)S(1)} %get-tuple-element.45), channel_id=1, source_target_pairs={{0,48},{16,0},{32,16},{48,32},{1,49},{17,1},{33,17},{49,33},{2,50}... | collective-permute-start | bytes 1572872 | tf_op jit(solution)/shard_map/ppermute | solution.py:23
  22.8 5.6 %collective-permute-done.10.refs_1_ = bf16[256,1024]{1,0:T(8,128)(2,1)S(1)} collective-permute-done((bf16[256,1024]{1,0:T(8,128)(2,1)S(1)}, bf16[256,1024]{1,0:T(8,128)(2,1)S(1)}, u32[]{:S(2)}, u32[]{:S(2)}) %collective-permute-start.10) | collective-permute-done | bytes 524320 | tf_op jit(solution)/shard_map/ppermute | solution.py:23
  28.4 0.7 slice.113
  29.1 1.1 collective-permute-start.11
  30.2 1.0 collective-permute-done.6.refs_0_
  31.2 0.7 slice.111
  31.9 0.7 slice.114
  32.6 0.8 copy-done.1
  33.4 0.9 collective-permute-start.13
  34.4 0.7 slice.112
  35.1 0.8 copy-done.3
  35.9 3.2 %collective-permute-start.9 = (bf16[128,1024]{1,0:T(8,128)(2,1)}, bf16[128,1024]{1,0:T(8,128)(2,1)}, u32[]{:S(2)}, u32[]{:S(2)}) collective-permute-start(bf16[128,1024]{1,0:T(8,128)(2,1)} %slice.112), channel_id=1, source_target_pairs={{0,48},{16,0},{32,16},{48,32},{1,49},{17,1},{33,17},{49,33},{2,50}... | collective-permute-start | bytes 786440 | tf_op jit(solution)/shard_map/ppermute | solution.py:23
  39.3 1.3 shard_map.93
  40.6 2.4 %shard_map.95 = (bf16[2048,1024]{1,0:T(8,128)(2,1)S(1)}, bf16[2048,1024]{1,0:T(8,128)(2,1)S(1)}, bf16[2048,1024]{1,0:T(8,128)(2,1)S(1)}) custom-call(s32[4]{0:T(128)S(1)} %pad_add_fusion.at, bf16[2048,128]{1,0:T(8,128)(2,1)S(1)} %get-tuple-element.41.hot, bf16[128,1024]{1,0:T(8,128)(2,1)S(1)} %get-tuple-element.42.factors, ...), custom_call_target="tpu_custom_call" | custom-call | tf_op jit(solution)/shard_map/pallas_call | solution.py:179
  43.0 4.2 %shard_map.96 = (bf16[2048,1024]{1,0:T(8,128)(2,1)S(1)}, bf16[2048,1024]{1,0:T(8,128)(2,1)S(1)}, bf16[2048,1024]{1,0:T(8,128)(2,1)S(1)}) custom-call(s32[4]{0:T(128)S(1)} %pad_add_fusion.at, bf16[2048,128]{1,0:T(8,128)(2,1)S(1)} %get-tuple-element.41.hot, ...), custom_call_target="tpu_custom_call", output_to_operand_aliasing={{0}: (8, {}), {1}: (9, {}), {2}: (10, {})} | custom-call | tf_op jit(solution)/shard_map/pallas_call | solution.py:179
  47.3 2.9 %shard_map.97 = (bf16[2048,1024]{1,0:T(8,128)(2,1)S(1)}, bf16[2048,1024]{1,0:T(8,128)(2,1)S(1)}, bf16[2048,1024]{1,0:T(8,128)(2,1)S(1)}) custom-call(s32[4]{0:T(128)S(1)} %pad_add_fusion.at, bf16[2048,128]{1,0:T(8,128)(2,1)S(1)} %get-tuple-element.41.hot, ...), custom_call_target="tpu_custom_call", output_to_operand_aliasing={{0}: (8, {}), {1}: (9, {}), {2}: (10, {})} | custom-call | tf_op jit(solution)/shard_map/pallas_call | solution.py:179
  50.2 0.4 fusion.2
  50.8 0.4 copy-done.9
  51.2 5.9 %collective-permute-start.22 = (bf16[128,1024]{1,0:T(8,128)(2,1)S(1)}, bf16[128,1024]{1,0:T(8,128)(2,1)S(1)}, u32[]{:S(2)}, u32[]{:S(2)}) collective-permute-start(bf16[128,1024]{1,0:T(8,128)(2,1)S(1)} %copy-done.9), channel_id=1, source_target_pairs={{0,14},{2,0},{4,2},{6,4},{8,6},{10,8},{12,10},{14,12},{1,15},{3,1}... | collective-permute-start | bytes 786440 | tf_op jit(solution)/shard_map/ppermute | solution.py:23
  57.1 5.8 %collective-permute-done.22.refs_1_ = bf16[128,1024]{1,0:T(8,128)(2,1)S(1)} collective-permute-done((bf16[128,1024]{1,0:T(8,128)(2,1)S(1)}, bf16[128,1024]{1,0:T(8,128)(2,1)S(1)}, u32[]{:S(2)}, u32[]{:S(2)}) %collective-permute-start.22) | collective-permute-done | bytes 262176 | tf_op jit(solution)/shard_map/ppermute | solution.py:23
  62.9 3.7 %collective-permute-start.23 = (bf16[128,1024]{1,0:T(8,128)(2,1)S(1)}, bf16[128,1024]{1,0:T(8,128)(2,1)S(1)}, u32[]{:S(2)}, u32[]{:S(2)}) collective-permute-start(bf16[128,1024]{1,0:T(8,128)(2,1)S(1)} %collective-permute-done.22.refs_1_), channel_id=1, source_target_pairs={{0,14},{2,0},{4,2},{6,4},{8,6},{10,8},{12,10},{14,12},{1,15},{3,1}... | collective-permute-start | bytes 786440 | tf_op jit(solution)/shard_map/ppermute | solution.py:23
  66.6 5.0 %collective-permute-done.23.refs_2_ = bf16[128,1024]{1,0:T(8,128)(2,1)S(1)} collective-permute-done((bf16[128,1024]{1,0:T(8,128)(2,1)S(1)}, bf16[128,1024]{1,0:T(8,128)(2,1)S(1)}, u32[]{:S(2)}, u32[]{:S(2)}) %collective-permute-start.23) | collective-permute-done | bytes 262176 | tf_op jit(solution)/shard_map/ppermute | solution.py:23
  71.6 3.4 %collective-permute-done.25.refs_3_ = bf16[128,1024]{1,0:T(8,128)(2,1)S(1)} collective-permute-done((bf16[128,1024]{1,0:T(8,128)(2,1)S(1)}, bf16[128,1024]{1,0:T(8,128)(2,1)S(1)}, u32[]{:S(2)}, u32[]{:S(2)}) %collective-permute-start.25) | collective-permute-done | bytes 262176 | tf_op jit(solution)/shard_map/ppermute | solution.py:23
  75.2 0.4 collective-permute-start.27
  75.5 1.7 %collective-permute-start.29 = (bf16[128,1024]{1,0:T(8,128)(2,1)S(1)}, bf16[128,1024]{1,0:T(8,128)(2,1)S(1)}, u32[]{:S(2)}, u32[]{:S(2)}) collective-permute-start(bf16[128,1024]{1,0:T(8,128)(2,1)S(1)} %collective-permute-done.25.refs_3_), channel_id=1, source_target_pairs={{0,2},{2,4},{4,6},{6,8},{8,10},{10,12},{12,14},{14,0},{1,3},{3,5},... | collective-permute-start | bytes 786440 | tf_op jit(solution)/shard_map/ppermute | solution.py:23
  77.3 6.6 %collective-permute-done.27.refs_0_ = bf16[128,1024]{1,0:T(8,128)(2,1)S(1)} collective-permute-done((bf16[128,1024]{1,0:T(8,128)(2,1)S(1)}, bf16[128,1024]{1,0:T(8,128)(2,1)S(1)}, u32[]{:S(2)}, u32[]{:S(2)}) %collective-permute-start.27) | collective-permute-done | bytes 262176 | tf_op jit(solution)/shard_map/ppermute | solution.py:23
  83.9 1.5 %collective-permute-start.28 = (bf16[128,1024]{1,0:T(8,128)(2,1)S(1)}, bf16[128,1024]{1,0:T(8,128)(2,1)S(1)}, u32[]{:S(2)}, u32[]{:S(2)}) collective-permute-start(bf16[128,1024]{1,0:T(8,128)(2,1)S(1)} %collective-permute-done.27.refs_0_), channel_id=1, source_target_pairs={{0,14},{2,0},{4,2},{6,4},{8,6},{10,8},{12,10},{14,12},{1,15},{3,1}... | collective-permute-start | bytes 786440 | tf_op jit(solution)/shard_map/ppermute | solution.py:23
  85.4 6.3 %collective-permute-done.28.refs_1_ = bf16[128,1024]{1,0:T(8,128)(2,1)S(1)} collective-permute-done((bf16[128,1024]{1,0:T(8,128)(2,1)S(1)}, bf16[128,1024]{1,0:T(8,128)(2,1)S(1)}, u32[]{:S(2)}, u32[]{:S(2)}) %collective-permute-start.28) | collective-permute-done | bytes 262176 | tf_op jit(solution)/shard_map/ppermute | solution.py:23
  91.8 0.2 add_convert_fusion.6
  92.0 0.3 collective-permute-start.15
  92.3 4.8 %shard_map.99 = (bf16[1280,1024]{1,0:T(8,128)(2,1)S(1)}, f32[16,1024]{1,0:T(8,128)S(1)}) custom-call(bf16[2048,128]{1,0:T(8,128)(2,1)S(1)} %get-tuple-element.41.hot, bf16[16,2048]{1,0:T(8,128)(2,1)S(1)} %get-tuple-element.71.hot_t, bf16[128,1024]{1,0:T(8,128)(2,1)S(1)} %get-tuple-element.70.factors, bf16[1024,1024]{1,0:T(8,128)(2,1)S(1)} %copy-done, ...), custom_call_target="tpu_custom_call" | custom-call | tf_op jit(solution)/shard_map/pallas_call | solution.py:179
  97.2 2.9 %shard_map.101 = (bf16[768,1024]{1,0:T(8,128)(2,1)S(1)}, f32[16,1024]{1,0:T(8,128)S(1)}) custom-call(bf16[2048,128]{1,0:T(8,128)(2,1)S(1)} %get-tuple-element.41.hot, bf16[16,2048]{1,0:T(8,128)(2,1)S(1)} %get-tuple-element.71.hot_t, bf16[128,1024]{1,0:T(8,128)(2,1)S(1)} %get-tuple-element.70.factors, bf16[1024,1024]{1,0:T(8,128)(2,1)S(1)} %copy-done, ...), custom_call_target="tpu_custom_call" | custom-call | tf_op jit(solution)/shard_map/pallas_call | solution.py:179
  100.1 2.9 %collective-permute-start.35 = (f32[8,1024]{1,0:T(8,128)S(1)}, f32[8,1024]{1,0:T(8,128)S(1)}, u32[]{:S(2)}, u32[]{:S(2)}) collective-permute-start(f32[8,1024]{1,0:T(8,128)S(1)} %slice.110), channel_id=1, source_target_pairs={{0,64},{64,0},{128,192},{192,128},{1,65},{65,1},{129,193},{193,129... | collective-permute-start | bytes 98312 | tf_op jit(solution)/shard_map/ppermute | solution.py:27
  102.9 2.2 %shard_map.104 = f32[16,1024]{1,0:T(8,128)S(1)} custom-call(bf16[16,2048]{1,0:T(8,128)(2,1)S(1)} %get-tuple-element.71.hot_t, bf16[2048,1024]{1,0:T(8,128)(2,1)S(1)} %get-tuple-element.54.back, bf16[640,1024]{1,0:T(8,128)(2,1)S(1)} %shard_map.98.own.refs_0_, bf16[640,1024]{1,0:T(8,128)(2,1)S(1)} %collective-permute-done.26.other.refs_1_, ...), custom_call_target="tpu_custom_call" | custom-call | tf_op jit(solution)/shard_map/pallas_call | solution.py:179
  105.1 0.3 collective-permute-start.31
  105.5 3.1 %collective-permute-start.19 = (bf16[128,1024]{1,0:T(8,128)(2,1)S(1)}, bf16[128,1024]{1,0:T(8,128)(2,1)S(1)}, u32[]{:S(2)}, u32[]{:S(2)}) collective-permute-start(bf16[128,1024]{1,0:T(8,128)(2,1)S(1)} %get-tuple-element.79), channel_id=1, source_target_pairs={{0,14},{2,0},{4,2},{6,4},{8,6},{10,8},{12,10},{14,12},{1,15},{3,1}... | collective-permute-start | bytes 786440 | tf_op jit(solution)/shard_map/ppermute | solution.py:23
  109.0 5.9 %collective-permute-done.19 = bf16[128,1024]{1,0:T(8,128)(2,1)S(1)} collective-permute-done((bf16[128,1024]{1,0:T(8,128)(2,1)S(1)}, bf16[128,1024]{1,0:T(8,128)(2,1)S(1)}, u32[]{:S(2)}, u32[]{:S(2)}) %collective-permute-start.19) | collective-permute-done | bytes 262176 | tf_op jit(solution)/shard_map/ppermute | solution.py:23
  115.0 3.8 %collective-permute-start.20 = (bf16[128,1024]{1,0:T(8,128)(2,1)S(1)}, bf16[128,1024]{1,0:T(8,128)(2,1)S(1)}, u32[]{:S(2)}, u32[]{:S(2)}) collective-permute-start(bf16[128,1024]{1,0:T(8,128)(2,1)S(1)} %add_convert_fusion.1), channel_id=1, source_target_pairs={{0,14},{2,0},{4,2},{6,4},{8,6},{10,8},{12,10},{14,12},{1,15},{3,1}... | collective-permute-start | bytes 786440 | tf_op jit(solution)/shard_map/ppermute | solution.py:23
  119.1 0.4 collective-permute-start.33
  119.5 4.6 %collective-permute-done.20 = bf16[128,1024]{1,0:T(8,128)(2,1)S(1)} collective-permute-done((bf16[128,1024]{1,0:T(8,128)(2,1)S(1)}, bf16[128,1024]{1,0:T(8,128)(2,1)S(1)}, u32[]{:S(2)}, u32[]{:S(2)}) %collective-permute-start.20) | collective-permute-done | bytes 262176 | tf_op jit(solution)/shard_map/ppermute | solution.py:23
  124.2 3.8 %collective-permute-start.21 = (bf16[128,1024]{1,0:T(8,128)(2,1)S(1)}, bf16[128,1024]{1,0:T(8,128)(2,1)S(1)}, u32[]{:S(2)}, u32[]{:S(2)}) collective-permute-start(bf16[128,1024]{1,0:T(8,128)(2,1)S(1)} %add_convert_fusion), channel_id=1, source_target_pairs={{0,14},{2,0},{4,2},{6,4},{8,6},{10,8},{12,10},{14,12},{1,15},{3,1}... | collective-permute-start | bytes 786440 | tf_op jit(solution)/shard_map/ppermute | solution.py:23
  128.2 1.4 collective-permute-start.38
  129.6 1.9 %collective-permute-start.34 = (f32[8,1024]{1,0:T(8,128)S(1)}, f32[8,1024]{1,0:T(8,128)S(1)}, u32[]{:S(2)}, u32[]{:S(2)}) collective-permute-start(f32[8,1024]{1,0:T(8,128)S(1)} %add.86), channel_id=1, source_target_pairs={{0,8},{2,10},{4,12},{6,14},{8,0},{10,2},{12,4},{14,6},{1,9},{3,11}... | collective-permute-start | bytes 98312 | tf_op jit(solution)/shard_map/ppermute | solution.py:27
  131.5 0.2 fusion
  131.8 3.9 %shard_map.102.refs_0_ = f32[1024,1024]{1,0:T(8,128)} custom-call(bf16[1280,1024]{1,0:T(8,128)(2,1)S(1)} %get-tuple-element.73.first, bf16[768,1024]{1,0:T(8,128)(2,1)S(1)} %get-tuple-element.75.second, bf16[2048,1024]{1,0:T(8,128)(2,1)S(1)} %get-tuple-element.76.scaled_cot), custom_call_target="tpu_custom_call" | custom-call | tf_op jit(solution)/shard_map/pallas_call | solution.py:163
  135.6 3.9 %shard_map.103 = f32[1024,1024]{1,0:T(8,128)} custom-call(bf16[1280,1024]{1,0:T(8,128)(2,1)S(1)} %get-tuple-element.73.first, bf16[768,1024]{1,0:T(8,128)(2,1)S(1)} %get-tuple-element.75.second, bf16[2048,1024]{1,0:T(8,128)(2,1)S(1)} %get-tuple-element.76.scaled_cot, f32[1024,1024]{1,0:T(8,128)} %shard_map.102.refs_0_), custom_call_target="tpu_custom_call", output_to_operand_aliasing={{}: (3, {})} | custom-call | tf_op jit(solution)/shard_map/pallas_call | solution.py:163
  139.5 0.6 add.91
  140.1 0.6 add.87
  140.8 0.9 multiply_convert_fusion
  (78 shorter events, 1.8 us)
Async XLA Ops:
  0.6 38.6 %copy-start.12 = (s32[2048]{0:T(1024)S(1)}, s32[2048]{0:T(1024)}, u32[]{:S(2)}) copy-start(s32[2048]{0:T(1024)} %param.11) | copy-start | bytes 24580
  0.6 38.6 %copy-start.11 = (f32[8,1024]{1,0:T(8,128)S(1)}, f32[8,1024]{1,0:T(8,128)}, u32[]{:S(2)}) copy-start(f32[8,1024]{1,0:T(8,128)} %scale_out.1) | copy-start | bytes 98308
  0.7 38.6 %copy-start = (bf16[1024,1024]{1,0:T(8,128)(2,1)S(1)}, bf16[1024,1024]{1,0:T(8,128)(2,1)}, u32[]{:S(2)}) copy-start(bf16[1024,1024]{1,0:T(8,128)(2,1)} %weight.5) | copy-start | bytes 6291460
  0.7 38.6 %copy-start.10 = (f32[8,1024]{1,0:T(8,128)S(1)}, f32[8,1024]{1,0:T(8,128)}, u32[]{:S(2)}) copy-start(f32[8,1024]{1,0:T(8,128)} %scale_in.1) | copy-start | bytes 98308
  1.8 7.6 %collective-permute-start = (bf16[64,1024]{1,0:T(8,128)(2,1)S(1)}, bf16[64,1024]{1,0:T(8,128)(2,1)S(1)}, u32[]{:S(2)}, u32[]{:S(2)}) collective-permute-start(bf16[64,1024]{1,0:T(8,128)(2,1)S(1)} %get-tuple-element.83.refs_0_), channel_id=1, source_target_pairs={{0,64},{64,128},{128,192},{192,0},{1,65},{65,129},{129,193},{193,1... | collective-permute-start | bytes 393224 | tf_op jit(solution)/shard_map/ppermute | solution.py:23
  3.4 7.9 %collective-permute-start.1 = (bf16[64,1024]{1,0:T(8,128)(2,1)S(1)}, bf16[64,1024]{1,0:T(8,128)(2,1)S(1)}, u32[]{:S(2)}, u32[]{:S(2)}) collective-permute-start(bf16[64,1024]{1,0:T(8,128)(2,1)S(1)} %get-tuple-element.83.refs_0_), channel_id=1, source_target_pairs={{0,192},{64,0},{128,64},{192,128},{1,193},{65,1},{129,65},{193,129... | collective-permute-start | bytes 393224 | tf_op jit(solution)/shard_map/ppermute | solution.py:23
  4.2 7.6 %collective-permute-start.2 = (bf16[64,1024]{1,0:T(8,128)(2,1)S(1)}, bf16[64,1024]{1,0:T(8,128)(2,1)S(1)}, u32[]{:S(2)}, u32[]{:S(2)}) collective-permute-start(bf16[64,1024]{1,0:T(8,128)(2,1)S(1)} %get-tuple-element.83.refs_0_), channel_id=1, source_target_pairs={{0,128},{64,192},{128,0},{192,64},{1,129},{65,193},{129,1},{193,65... | collective-permute-start | bytes 393224 | tf_op jit(solution)/shard_map/ppermute | solution.py:23
  6.2 6.9 %collective-permute-start.3 = (bf16[64,1024]{1,0:T(8,128)(2,1)S(1)}, bf16[64,1024]{1,0:T(8,128)(2,1)S(1)}, u32[]{:S(2)}, u32[]{:S(2)}) collective-permute-start(bf16[64,1024]{1,0:T(8,128)(2,1)S(1)} %get-tuple-element.82.refs_4_), channel_id=1, source_target_pairs={{0,16},{16,32},{32,48},{48,0},{1,17},{17,33},{33,49},{49,1},{2,18}... | collective-permute-start | bytes 393224 | tf_op jit(solution)/shard_map/ppermute | solution.py:23
  7.6 6.1 %collective-permute-start.4 = (bf16[64,1024]{1,0:T(8,128)(2,1)S(1)}, bf16[64,1024]{1,0:T(8,128)(2,1)S(1)}, u32[]{:S(2)}, u32[]{:S(2)}) collective-permute-start(bf16[64,1024]{1,0:T(8,128)(2,1)S(1)} %get-tuple-element.82.refs_4_), channel_id=1, source_target_pairs={{0,48},{16,0},{32,16},{48,32},{1,49},{17,1},{33,17},{49,33},{2,50}... | collective-permute-start | bytes 393224 | tf_op jit(solution)/shard_map/ppermute | solution.py:23
  9.4 6.6 %collective-permute-start.5 = (bf16[64,1024]{1,0:T(8,128)(2,1)S(1)}, bf16[64,1024]{1,0:T(8,128)(2,1)S(1)}, u32[]{:S(2)}, u32[]{:S(2)}) collective-permute-start(bf16[64,1024]{1,0:T(8,128)(2,1)S(1)} %get-tuple-element.82.refs_4_), channel_id=1, source_target_pairs={{0,32},{16,48},{32,0},{48,16},{1,33},{17,49},{33,1},{49,17},{2,34}... | collective-permute-start | bytes 393224 | tf_op jit(solution)/shard_map/ppermute | solution.py:23
  16.2 18.9 %copy-start.5 = (bf16[256,1024]{1,0:T(8,128)(2,1)}, bf16[256,1024]{1,0:T(8,128)(2,1)S(1)}, u32[]{:S(2)}) copy-start(bf16[256,1024]{1,0:T(8,128)(2,1)S(1)} %get-tuple-element.44.refs_0_) | copy-start | bytes 1572868
  16.2 12.1 %collective-permute-start.10 = (bf16[256,1024]{1,0:T(8,128)(2,1)S(1)}, bf16[256,1024]{1,0:T(8,128)(2,1)S(1)}, u32[]{:S(2)}, u32[]{:S(2)}) collective-permute-start(bf16[256,1024]{1,0:T(8,128)(2,1)S(1)} %get-tuple-element.46.refs_1_), channel_id=1, source_target_pairs={{0,64},{64,128},{128,192},{192,0},{1,65},{65,129},{129,193},{193,1... | collective-permute-start | bytes 1572872 | tf_op jit(solution)/shard_map/ppermute | solution.py:23
  18.8 0.8 copy-start.7
  19.6 11.6 %collective-permute-start.6 = (bf16[256,1024]{1,0:T(8,128)(2,1)S(1)}, bf16[256,1024]{1,0:T(8,128)(2,1)S(1)}, u32[]{:S(2)}, u32[]{:S(2)}) collective-permute-start(bf16[256,1024]{1,0:T(8,128)(2,1)S(1)} %get-tuple-element.44.refs_0_), channel_id=1, source_target_pairs={{0,16},{16,32},{32,48},{48,0},{1,17},{17,33},{33,49},{49,1},{2,18}... | collective-permute-start | bytes 1572872 | tf_op jit(solution)/shard_map/ppermute | solution.py:23
  19.6 12.3 %collective-permute-start.12 = (bf16[256,1024]{1,0:T(8,128)(2,1)S(1)}, bf16[256,1024]{1,0:T(8,128)(2,1)S(1)}, u32[]{:S(2)}, u32[]{:S(2)}) collective-permute-start(bf16[256,1024]{1,0:T(8,128)(2,1)S(1)} %get-tuple-element.47), channel_id=1, source_target_pairs={{0,192},{64,0},{128,64},{192,128},{1,193},{65,1},{129,65},{193,129... | collective-permute-start | bytes 1572872 | tf_op jit(solution)/shard_map/ppermute | solution.py:23
  19.9 14.5 %collective-permute-start.8 = (bf16[256,1024]{1,0:T(8,128)(2,1)S(1)}, bf16[256,1024]{1,0:T(8,128)(2,1)S(1)}, u32[]{:S(2)}, u32[]{:S(2)}) collective-permute-start(bf16[256,1024]{1,0:T(8,128)(2,1)S(1)} %get-tuple-element.45), channel_id=1, source_target_pairs={{0,48},{16,0},{32,16},{48,32},{1,49},{17,1},{33,17},{49,33},{2,50}... | collective-permute-start | bytes 1572872 | tf_op jit(solution)/shard_map/ppermute | solution.py:23
  29.1 18.1 %collective-permute-start.11 = (bf16[128,1024]{1,0:T(8,128)(2,1)}, bf16[128,1024]{1,0:T(8,128)(2,1)S(1)}, u32[]{:S(2)}, u32[]{:S(2)}) collective-permute-start(bf16[128,1024]{1,0:T(8,128)(2,1)} %slice.113), channel_id=1, source_target_pairs={{0,64},{64,128},{128,192},{192,0},{1,65},{65,129},{129,193},{193,1... | collective-permute-start | bytes 786440 | tf_op jit(solution)/shard_map/ppermute | solution.py:23
  31.9 15.3 %collective-permute-start.7 = (bf16[128,1024]{1,0:T(8,128)(2,1)}, bf16[128,1024]{1,0:T(8,128)(2,1)}, u32[]{:S(2)}, u32[]{:S(2)}) collective-permute-start(bf16[128,1024]{1,0:T(8,128)(2,1)} %slice.111), channel_id=1, source_target_pairs={{0,16},{16,32},{32,48},{48,0},{1,17},{17,33},{33,49},{49,1},{2,18}... | collective-permute-start | bytes 786440 | tf_op jit(solution)/shard_map/ppermute | solution.py:23
  32.6 0.8 copy-start.1
  33.4 13.8 %collective-permute-start.13 = (bf16[128,1024]{1,0:T(8,128)(2,1)}, bf16[128,1024]{1,0:T(8,128)(2,1)}, u32[]{:S(2)}, u32[]{:S(2)}) collective-permute-start(bf16[128,1024]{1,0:T(8,128)(2,1)} %slice.114), channel_id=1, source_target_pairs={{0,192},{64,0},{128,64},{192,128},{1,193},{65,1},{129,65},{193,129... | collective-permute-start | bytes 786440 | tf_op jit(solution)/shard_map/ppermute | solution.py:23
  35.1 0.8 copy-start.3
  35.9 11.4 %collective-permute-start.9 = (bf16[128,1024]{1,0:T(8,128)(2,1)}, bf16[128,1024]{1,0:T(8,128)(2,1)}, u32[]{:S(2)}, u32[]{:S(2)}) collective-permute-start(bf16[128,1024]{1,0:T(8,128)(2,1)} %slice.112), channel_id=1, source_target_pairs={{0,48},{16,0},{32,16},{48,32},{1,49},{17,1},{33,17},{49,33},{2,50}... | collective-permute-start | bytes 786440 | tf_op jit(solution)/shard_map/ppermute | solution.py:23
  39.2 1.5 %copy-start.6 = (bf16[256,1024]{1,0:T(8,128)(2,1)S(1)}, bf16[256,1024]{1,0:T(8,128)(2,1)}, u32[]{:S(2)}) copy-start(bf16[256,1024]{1,0:T(8,128)(2,1)} %copy-done.5) | copy-start | bytes 1572868
  39.2 1.5 %copy-start.8 = (bf16[256,1024]{1,0:T(8,128)(2,1)S(1)}, bf16[256,1024]{1,0:T(8,128)(2,1)}, u32[]{:S(2)}) copy-start(bf16[256,1024]{1,0:T(8,128)(2,1)} %copy-done.7) | copy-start | bytes 1572868
  40.6 2.4 %copy-start.2 = (bf16[256,1024]{1,0:T(8,128)(2,1)S(1)}, bf16[256,1024]{1,0:T(8,128)(2,1)}, u32[]{:S(2)}) copy-start(bf16[256,1024]{1,0:T(8,128)(2,1)} %copy-done.1) | copy-start | bytes 1572868
  40.6 2.4 %copy-start.4 = (bf16[256,1024]{1,0:T(8,128)(2,1)S(1)}, bf16[256,1024]{1,0:T(8,128)(2,1)}, u32[]{:S(2)}) copy-start(bf16[256,1024]{1,0:T(8,128)(2,1)} %copy-done.3) | copy-start | bytes 1572868
  50.2 1.0 copy-start.9
  50.7 41.1 %collective-permute-start.14 = (bf16[1024,1024]{1,0:T(8,128)(2,1)S(1)}, bf16[1024,1024]{1,0:T(8,128)(2,1)S(1)}, u32[]{:S(2)}, u32[]{:S(2)}) collective-permute-start(bf16[1024,1024]{1,0:T(8,128)(2,1)S(1)} %get-tuple-element.81), channel_id=1, source_target_pairs={{0,1},{1,0},{2,3},{3,2},{4,5},{5,4},{6,7},{7,6},{8,9},{9,8},{10,11... | collective-permute-start | bytes 6291464 | tf_op jit(solution)/shard_map/ppermute | solution.py:27
  51.2 11.7 %collective-permute-start.22 = (bf16[128,1024]{1,0:T(8,128)(2,1)S(1)}, bf16[128,1024]{1,0:T(8,128)(2,1)S(1)}, u32[]{:S(2)}, u32[]{:S(2)}) collective-permute-start(bf16[128,1024]{1,0:T(8,128)(2,1)S(1)} %copy-done.9), channel_id=1, source_target_pairs={{0,14},{2,0},{4,2},{6,4},{8,6},{10,8},{12,10},{14,12},{1,15},{3,1}... | collective-permute-start | bytes 786440 | tf_op jit(solution)/shard_map/ppermute | solution.py:23
  57.0 9.5 %collective-permute-start.24 = (bf16[128,1024]{1,0:T(8,128)(2,1)S(1)}, bf16[128,1024]{1,0:T(8,128)(2,1)S(1)}, u32[]{:S(2)}, u32[]{:S(2)}) collective-permute-start(bf16[128,1024]{1,0:T(8,128)(2,1)S(1)} %copy-done.9), channel_id=1, source_target_pairs={{0,2},{2,4},{4,6},{6,8},{8,10},{10,12},{12,14},{14,0},{1,3},{3,5},... | collective-permute-start | bytes 786440 | tf_op jit(solution)/shard_map/ppermute | solution.py:23
  62.9 8.7 %collective-permute-start.23 = (bf16[128,1024]{1,0:T(8,128)(2,1)S(1)}, bf16[128,1024]{1,0:T(8,128)(2,1)S(1)}, u32[]{:S(2)}, u32[]{:S(2)}) collective-permute-start(bf16[128,1024]{1,0:T(8,128)(2,1)S(1)} %collective-permute-done.22.refs_1_), channel_id=1, source_target_pairs={{0,14},{2,0},{4,2},{6,4},{8,6},{10,8},{12,10},{14,12},{1,15},{3,1}... | collective-permute-start | bytes 786440 | tf_op jit(solution)/shard_map/ppermute | solution.py:23
  66.6 8.4 %collective-permute-start.25 = (bf16[128,1024]{1,0:T(8,128)(2,1)S(1)}, bf16[128,1024]{1,0:T(8,128)(2,1)S(1)}, u32[]{:S(2)}, u32[]{:S(2)}) collective-permute-start(bf16[128,1024]{1,0:T(8,128)(2,1)S(1)} %collective-permute-done.24.refs_4_), channel_id=1, source_target_pairs={{0,2},{2,4},{4,6},{6,8},{8,10},{10,12},{12,14},{14,0},{1,3},{3,5},... | collective-permute-start | bytes 786440 | tf_op jit(solution)/shard_map/ppermute | solution.py:23
  75.1 17.2 %collective-permute-start.26 = (bf16[640,1024]{1,0:T(8,128)(2,1)S(1)}, bf16[640,1024]{1,0:T(8,128)(2,1)S(1)}, u32[]{:S(2)}, u32[]{:S(2)}) collective-permute-start(bf16[640,1024]{1,0:T(8,128)(2,1)S(1)} %shard_map.98.own.refs_0_), channel_id=1, source_target_pairs={{0,1},{1,0},{2,3},{3,2},{4,5},{5,4},{6,7},{7,6},{8,9},{9,8},{10,11... | collective-permute-start | bytes 3932168 | tf_op jit(solution)/shard_map/ppermute | solution.py:27
  75.2 8.7 %collective-permute-start.27 = (bf16[128,1024]{1,0:T(8,128)(2,1)S(1)}, bf16[128,1024]{1,0:T(8,128)(2,1)S(1)}, u32[]{:S(2)}, u32[]{:S(2)}) collective-permute-start(bf16[128,1024]{1,0:T(8,128)(2,1)S(1)} %collective-permute-done.23.refs_2_), channel_id=1, source_target_pairs={{0,14},{2,0},{4,2},{6,4},{8,6},{10,8},{12,10},{14,12},{1,15},{3,1}... | collective-permute-start | bytes 786440 | tf_op jit(solution)/shard_map/ppermute | solution.py:23
  75.5 9.8 %collective-permute-start.29 = (bf16[128,1024]{1,0:T(8,128)(2,1)S(1)}, bf16[128,1024]{1,0:T(8,128)(2,1)S(1)}, u32[]{:S(2)}, u32[]{:S(2)}) collective-permute-start(bf16[128,1024]{1,0:T(8,128)(2,1)S(1)} %collective-permute-done.25.refs_3_), channel_id=1, source_target_pairs={{0,2},{2,4},{4,6},{6,8},{8,10},{10,12},{12,14},{14,0},{1,3},{3,5},... | collective-permute-start | bytes 786440 | tf_op jit(solution)/shard_map/ppermute | solution.py:23
  83.9 7.8 %collective-permute-start.28 = (bf16[128,1024]{1,0:T(8,128)(2,1)S(1)}, bf16[128,1024]{1,0:T(8,128)(2,1)S(1)}, u32[]{:S(2)}, u32[]{:S(2)}) collective-permute-start(bf16[128,1024]{1,0:T(8,128)(2,1)S(1)} %collective-permute-done.27.refs_0_), channel_id=1, source_target_pairs={{0,14},{2,0},{4,2},{6,4},{8,6},{10,8},{12,10},{14,12},{1,15},{3,1}... | collective-permute-start | bytes 786440 | tf_op jit(solution)/shard_map/ppermute | solution.py:23
  91.7 5.5 %collective-permute-start.30 = (bf16[384,1024]{1,0:T(8,128)(2,1)S(1)}, bf16[384,1024]{1,0:T(8,128)(2,1)S(1)}, u32[]{:S(2)}, u32[]{:S(2)}) collective-permute-start(bf16[384,1024]{1,0:T(8,128)(2,1)S(1)} %shard_map.100.own.refs_2_), channel_id=1, source_target_pairs={{0,1},{1,0},{2,3},{3,2},{4,5},{5,4},{6,7},{7,6},{8,9},{9,8},{10,11... | collective-permute-start | bytes 2359304 | tf_op jit(solution)/shard_map/ppermute | solution.py:27
  92.0 16.6 %collective-permute-start.15 = (bf16[128,1024]{1,0:T(8,128)(2,1)S(1)}, bf16[128,1024]{1,0:T(8,128)(2,1)S(1)}, u32[]{:S(2)}, u32[]{:S(2)}) collective-permute-start(bf16[128,1024]{1,0:T(8,128)(2,1)S(1)} %get-tuple-element.78), channel_id=1, source_target_pairs={{0,2},{2,4},{4,6},{6,8},{8,10},{10,12},{12,14},{14,0},{1,3},{3,5},... | collective-permute-start | bytes 786440 | tf_op jit(solution)/shard_map/ppermute | solution.py:23
  100.1 5.3 %collective-permute-start.35 = (f32[8,1024]{1,0:T(8,128)S(1)}, f32[8,1024]{1,0:T(8,128)S(1)}, u32[]{:S(2)}, u32[]{:S(2)}) collective-permute-start(f32[8,1024]{1,0:T(8,128)S(1)} %slice.110), channel_id=1, source_target_pairs={{0,64},{64,0},{128,192},{192,128},{1,65},{65,1},{129,193},{193,129... | collective-permute-start | bytes 98312 | tf_op jit(solution)/shard_map/ppermute | solution.py:27
  105.1 3.7 %collective-permute-start.31 = (f32[8,1024]{1,0:T(8,128)S(1)}, f32[8,1024]{1,0:T(8,128)S(1)}, u32[]{:S(2)}, u32[]{:S(2)}) collective-permute-start(f32[8,1024]{1,0:T(8,128)S(1)} %slice.118), channel_id=1, source_target_pairs={{0,1},{1,0},{2,3},{3,2},{4,5},{5,4},{6,7},{7,6},{8,9},{9,8},{10,11... | collective-permute-start | bytes 98312 | tf_op jit(solution)/shard_map/ppermute | solution.py:27
  105.4 13.5 %collective-permute-start.36 = (f32[8,1024]{1,0:T(8,128)S(1)}, f32[8,1024]{1,0:T(8,128)S(1)}, u32[]{:S(2)}, u32[]{:S(2)}) collective-permute-start(f32[8,1024]{1,0:T(8,128)S(1)} %slice_add_fusion.1), channel_id=1, source_target_pairs={{0,16},{16,0},{32,48},{48,32},{1,17},{17,1},{33,49},{49,33},{2,18}... | collective-permute-start | bytes 98312 | tf_op jit(solution)/shard_map/ppermute | solution.py:27
  105.5 9.3 %collective-permute-start.19 = (bf16[128,1024]{1,0:T(8,128)(2,1)S(1)}, bf16[128,1024]{1,0:T(8,128)(2,1)S(1)}, u32[]{:S(2)}, u32[]{:S(2)}) collective-permute-start(bf16[128,1024]{1,0:T(8,128)(2,1)S(1)} %get-tuple-element.79), channel_id=1, source_target_pairs={{0,14},{2,0},{4,2},{6,4},{8,6},{10,8},{12,10},{14,12},{1,15},{3,1}... | collective-permute-start | bytes 786440 | tf_op jit(solution)/shard_map/ppermute | solution.py:23
  108.8 10.0 %collective-permute-start.16 = (bf16[128,1024]{1,0:T(8,128)(2,1)S(1)}, bf16[128,1024]{1,0:T(8,128)(2,1)S(1)}, u32[]{:S(2)}, u32[]{:S(2)}) collective-permute-start(bf16[128,1024]{1,0:T(8,128)(2,1)S(1)} %add_convert_fusion.5), channel_id=1, source_target_pairs={{0,2},{2,4},{4,6},{6,8},{8,10},{10,12},{12,14},{14,0},{1,3},{3,5},... | collective-permute-start | bytes 786440 | tf_op jit(solution)/shard_map/ppermute | solution.py:23
  108.9 10.2 %collective-permute-start.32 = (f32[8,1024]{1,0:T(8,128)S(1)}, f32[8,1024]{1,0:T(8,128)S(1)}, u32[]{:S(2)}, u32[]{:S(2)}) collective-permute-start(f32[8,1024]{1,0:T(8,128)S(1)} %slice_add_fusion), channel_id=1, source_target_pairs={{0,2},{2,0},{4,6},{6,4},{8,10},{10,8},{12,14},{14,12},{1,3},{3,1},... | collective-permute-start | bytes 98312 | tf_op jit(solution)/shard_map/ppermute | solution.py:27
  115.0 9.1 %collective-permute-start.20 = (bf16[128,1024]{1,0:T(8,128)(2,1)S(1)}, bf16[128,1024]{1,0:T(8,128)(2,1)S(1)}, u32[]{:S(2)}, u32[]{:S(2)}) collective-permute-start(bf16[128,1024]{1,0:T(8,128)(2,1)S(1)} %add_convert_fusion.1), channel_id=1, source_target_pairs={{0,14},{2,0},{4,2},{6,4},{8,6},{10,8},{12,10},{14,12},{1,15},{3,1}... | collective-permute-start | bytes 786440 | tf_op jit(solution)/shard_map/ppermute | solution.py:23
  118.9 9.1 %collective-permute-start.17 = (bf16[128,1024]{1,0:T(8,128)(2,1)S(1)}, bf16[128,1024]{1,0:T(8,128)(2,1)S(1)}, u32[]{:S(2)}, u32[]{:S(2)}) collective-permute-start(bf16[128,1024]{1,0:T(8,128)(2,1)S(1)} %add_convert_fusion.4), channel_id=1, source_target_pairs={{0,2},{2,4},{4,6},{6,8},{8,10},{10,12},{12,14},{14,0},{1,3},{3,5},... | collective-permute-start | bytes 786440 | tf_op jit(solution)/shard_map/ppermute | solution.py:23
  119.0 9.2 %collective-permute-start.37 = (f32[8,1024]{1,0:T(8,128)S(1)}, f32[8,1024]{1,0:T(8,128)S(1)}, u32[]{:S(2)}, u32[]{:S(2)}) collective-permute-start(f32[8,1024]{1,0:T(8,128)S(1)} %add.89), channel_id=1, source_target_pairs={{0,128},{64,192},{128,0},{192,64},{1,129},{65,193},{129,1},{193,65... | collective-permute-start | bytes 98312 | tf_op jit(solution)/shard_map/ppermute | solution.py:27
  119.1 10.5 %collective-permute-start.33 = (f32[8,1024]{1,0:T(8,128)S(1)}, f32[8,1024]{1,0:T(8,128)S(1)}, u32[]{:S(2)}, u32[]{:S(2)}) collective-permute-start(f32[8,1024]{1,0:T(8,128)S(1)} %add.85), channel_id=1, source_target_pairs={{0,4},{2,6},{4,0},{6,2},{8,12},{10,14},{12,8},{14,10},{1,5},{3,7},... | collective-permute-start | bytes 98312 | tf_op jit(solution)/shard_map/ppermute | solution.py:27
  124.2 16.5 %collective-permute-start.21 = (bf16[128,1024]{1,0:T(8,128)(2,1)S(1)}, bf16[128,1024]{1,0:T(8,128)(2,1)S(1)}, u32[]{:S(2)}, u32[]{:S(2)}) collective-permute-start(bf16[128,1024]{1,0:T(8,128)(2,1)S(1)} %add_convert_fusion), channel_id=1, source_target_pairs={{0,14},{2,0},{4,2},{6,4},{8,6},{10,8},{12,10},{14,12},{1,15},{3,1}... | collective-permute-start | bytes 786440 | tf_op jit(solution)/shard_map/ppermute | solution.py:23
  128.1 12.6 %collective-permute-start.18 = (bf16[128,1024]{1,0:T(8,128)(2,1)S(1)}, bf16[128,1024]{1,0:T(8,128)(2,1)S(1)}, u32[]{:S(2)}, u32[]{:S(2)}) collective-permute-start(bf16[128,1024]{1,0:T(8,128)(2,1)S(1)} %add_convert_fusion.3), channel_id=1, source_target_pairs={{0,2},{2,4},{4,6},{6,8},{8,10},{10,12},{12,14},{14,0},{1,3},{3,5},... | collective-permute-start | bytes 786440 | tf_op jit(solution)/shard_map/ppermute | solution.py:23
  128.2 11.3 %collective-permute-start.38 = (f32[8,1024]{1,0:T(8,128)S(1)}, f32[8,1024]{1,0:T(8,128)S(1)}, u32[]{:S(2)}, u32[]{:S(2)}) collective-permute-start(f32[8,1024]{1,0:T(8,128)S(1)} %add.90), channel_id=1, source_target_pairs={{0,32},{16,48},{32,0},{48,16},{1,33},{17,49},{33,1},{49,17},{2,34}... | collective-permute-start | bytes 98312 | tf_op jit(solution)/shard_map/ppermute | solution.py:27
  129.6 10.5 %collective-permute-start.34 = (f32[8,1024]{1,0:T(8,128)S(1)}, f32[8,1024]{1,0:T(8,128)S(1)}, u32[]{:S(2)}, u32[]{:S(2)}) collective-permute-start(f32[8,1024]{1,0:T(8,128)S(1)} %add.86), channel_id=1, source_target_pairs={{0,8},{2,10},{4,12},{6,14},{8,0},{10,2},{12,4},{14,6},{1,9},{3,11}... | collective-permute-start | bytes 98312 | tf_op jit(solution)/shard_map/ppermute | solution.py:27
